TPU v7x, 64 devices: a 2x2x8 block of a 4x4x8 slice. The times are simulated.
64 devices in a mesh: data: 4 (over x, y), seq: 16 (over z, core).
Axes of the slice: x: 2, y: 2, z: 8, core: 2. Of those that a mesh axis runs over, the one named last changes fastest.
The devices are a block of a 4x4x8 slice.
Arguments:
- x_in: bfloat16 [16384, 2560], P(('data', 'seq')), parts along dimension 0
- g_attn: float32 [2560], replicated
- w_qkv: bfloat16 [2560, 7680], replicated
- w_out: bfloat16 [32, 80, 2560], replicated
- g_mlp: float32 [2560], replicated
- w_gate: bfloat16 [2560, 10240], replicated
- w_up: bfloat16 [2560, 10240], replicated
- w_down: bfloat16 [10240, 2560], replicated
Outputs:
- output: bfloat16 [16384, 2560], P(('data', 'seq')), parts along dimension 0
There are 4 independent parts. A program takes and returns all parts, laid end to end along the dimension named above; an argument that names none is the same for every part.
All inputs are finite; a program needn't handle non-finite values.
Results may differ from a plain program's by a relative error of at most 0.00722409.
Values are sent between devices in bfloat16 or wider.
A program may use at most 768 MiB of HBM per device.

v0:
```python
import jax
import jax.numpy as jnp
from jax import lax
from jax.sharding import PartitionSpec as P

ROPE_BASE = 10000


def rms_norm(row_vals, gain_vec):
    rows_f32 = row_vals.astype(jnp.float32)
    inv_rms = lax.rsqrt(jnp.mean(rows_f32 * rows_f32, axis=-1, keepdims=True) + 1e-5)
    return (rows_f32 * inv_rms * gain_vec).astype(jnp.bfloat16)


def rope_tables(positions, head_dim):
    inv_freq = 1.0 / (ROPE_BASE ** (jnp.arange(0, head_dim, 2, dtype=jnp.float32) / head_dim))
    angles = positions.astype(jnp.float32)[:, None] * inv_freq[None, :]
    angles = jnp.concatenate([angles, angles], axis=-1)
    return jnp.cos(angles), jnp.sin(angles)


def apply_rope(qk_pair, cos_tab, sin_tab):
    half_dim = qk_pair.shape[-1] // 2
    rotated = jnp.concatenate([-qk_pair[..., half_dim:], qk_pair[..., :half_dim]], axis=-1)
    return qk_pair * cos_tab + rotated * sin_tab


def gated_mlp(y_rows, g_mlp, w_gate, w_up, w_down):
    y_norm = rms_norm(y_rows, g_mlp)
    gate_pre = jnp.dot(y_norm, w_gate, preferred_element_type=jnp.float32)
    up_pre = jnp.dot(y_norm, w_up, preferred_element_type=jnp.float32)
    hidden = (jax.nn.silu(gate_pre) * up_pre).astype(jnp.bfloat16)
    return (y_rows.astype(jnp.float32) + jnp.dot(hidden, w_down, preferred_element_type=jnp.float32)).astype(jnp.bfloat16)


def causal_attention(packed, block_rows):
    total_rows = packed.shape[0]
    local_heads = packed.shape[2]
    head_dim = packed.shape[3]
    query_rows = packed[:, 0]
    key_rows = packed[:, 1]
    value_rows = packed[:, 2]
    score_scale = head_dim ** -0.5
    key_pos = jnp.arange(total_rows)

    def one_block(block_idx):
        row_start = block_idx * block_rows
        q_blk = lax.dynamic_slice_in_dim(query_rows, row_start, block_rows, axis=0)
        scores = jnp.einsum('qhd,khd->hqk', q_blk, key_rows, preferred_element_type=jnp.float32) * score_scale
        query_pos = row_start + jnp.arange(block_rows)
        allowed = key_pos[None, :] <= query_pos[:, None]
        scores = jnp.where(allowed[None], scores, -jnp.inf)
        attn_probs = jax.nn.softmax(scores, axis=-1).astype(jnp.bfloat16)
        return jnp.einsum('hqk,khd->qhd', attn_probs, value_rows, preferred_element_type=jnp.float32).astype(jnp.bfloat16)

    blocks = lax.map(one_block, jnp.arange(total_rows // block_rows))
    return blocks.reshape(total_rows, local_heads, head_dim)


def solution(mesh):
    def local_layer(x_blk, g_attn, w_qkv, w_out, g_mlp, w_gate, w_up, w_down):
        n_heads, head_dim, model_width = w_out.shape
        local_rows = x_blk.shape[0]
        member = lax.axis_index('seq')
        x_norm = rms_norm(x_blk, g_attn)
        qkv_f32 = jnp.dot(x_norm, w_qkv, preferred_element_type=jnp.float32).reshape(local_rows, 3, n_heads, head_dim)
        positions = member * local_rows + jnp.arange(local_rows)
        cos_tab, sin_tab = rope_tables(positions, head_dim)
        qk_rot = apply_rope(qkv_f32[:, :2], cos_tab[:, None, None, :], sin_tab[:, None, None, :])
        packed = jnp.concatenate([qk_rot, qkv_f32[:, 2:]], axis=1).astype(jnp.bfloat16)
        head_major = lax.all_to_all(packed, 'seq', 2, 0, tiled=True)
        attn_heads = causal_attention(head_major, local_rows)
        attn_rows = lax.all_to_all(attn_heads, 'seq', 0, 1, tiled=True)
        attn_mixed = jnp.dot(attn_rows.reshape(local_rows, n_heads * head_dim), w_out.reshape(n_heads * head_dim, model_width), preferred_element_type=jnp.float32)
        y_rows = (x_blk.astype(jnp.float32) + attn_mixed).astype(jnp.bfloat16)
        return gated_mlp(y_rows, g_mlp, w_gate, w_up, w_down)

    row_spec = P(('data', 'seq'), None)
    return jax.shard_map(local_layer, mesh=mesh, in_specs=(row_spec, P(), P(), P(), P(), P(), P(), P()), out_specs=row_spec, check_vma=False)
```

profile of v0, /device:TPU:21, one launch (start us, length us, event | category | flops | bytes accessed | tf_op | source)
XLA Modules:
  0.0 491.1 jit_solution(14469082417223166920)
XLA Ops:
  1.7 23.0 %fusion.56 = f32[256,7680]{0,1:T(8,128)} fusion(bf16[2560,7680]{1,0:T(8,128)(2,1)} %param.12, bf16[256,2560]{1,0:T(8,128)(2,1)} %param.10, f32[2560]{0:T(1024)} %param.11, f32[256]{0:T(256)S(1)} %add_rsqrt_fusion.1), kind=kOutput, calls=%fused_computation.57 | convolution fusion | flops 10068951040 | bytes 48507904 | tf_op jit(solution)/shard_map/dot_general | solution.py:66
  24.7 4.6 slice_negate_fusion
  38.9 10.7 %all-to-all-start = ((bf16[256,3,32,80]{0,3,1,2:T(8,128)(2,1)}), bf16[256,3,32,80]{0,3,1,2:T(8,128)(2,1)}, u32[]{:S(2)}, u32[]{:S(2)}) async-start(bf16[256,3,32,80]{0,3,1,2:T(8,128)(2,1)} %copy.20), calls=%async_computation | async-start | bytes 7864320 | tf_op jit(solution)/shard_map/all_to_all | solution.py:71
  49.6 87.2 %all-to-all-done = bf16[256,3,32,80]{0,3,1,2:T(8,128)(2,1)} async-done(((bf16[256,3,32,80]{0,3,1,2:T(8,128)(2,1)}), bf16[256,3,32,80]{0,3,1,2:T(8,128)(2,1)}, u32[]{:S(2)}, u32[]{:S(2)}) %all-to-all-start) | async-done | bytes 3932192 | tf_op jit(solution)/shard_map/all_to_all | solution.py:71
  136.8 6.2 %copy.21 = bf16[16,256,3,2,80]{1,0,4,3,2:T(8,128)(2,1)} copy(bf16[16,256,3,2,80]{1,4,2,3,0:T(8,128)(2,1)} %bitcast.2) | data formatting | bytes 7864320 | tf_op jit(solution)/shard_map/all_to_all | solution.py:71
  143.1 7.1 %all_to_all.27 = bf16[4096,3,2,80]{0,3,2,1:T(8,128)(2,1)} reshape(bf16[16,256,3,2,80]{1,0,4,3,2:T(8,128)(2,1)} %copy.21) | data formatting | bytes 7864320 | tf_op jit(solution)/shard_map/all_to_all | solution.py:71
  154.4 186.5 %while.11 = (s32[]{:T(128)}, bf16[16,256,2,80]{1,3,2,0:T(8,128)(2,1)S(1)}, s32[16]{0:T(128)S(1)}, bf16[4096,2,80]{0,2,1:T(8,128)(2,1)}, bf16[4096,2,80]{0,2,1:T(...) while((s32[]{:T(128)}, ...), condition=%wide.region_4.5_spmd.clone, body=%wide.region_1.4_spmd.clone.sunk | while | flops 1026605824 | bytes 7330475 | solution.py:56
  160.7 5.2 %fusion.102 = bf16[16,256,2,80]{1,3,2,0:T(8,128)(2,1)S(1)} fusion(bf16[16,256,2,80]{1,3,2,0:T(8,128)(2,1)S(1)} %get-tuple-element.126, s32[]{:T(128)} %get-tuple-element.125, bf16[4096,2,80]{0,2,1:T(8,128)(2,1)} %get-tuple-element.140, f32[2,256]{1,0:T(2,128)S(1)} %fusion.101, pred[256,4096]{1,0:T(8,128)(4,1)S(1)} %iota_compare_fusion.2, ...), kind=kOutput, calls=%fused_computation.14.clone.1 | convolution fusion | flops 681619968 | bytes 3836420 | tf_op jit(solution)/shard_map/while/body/eval_jaxpr/hqk,khd->qhd/dot_general | solution.py:54
  167.9 4.4 fusion.101
  172.4 5.2 %fusion.102 = bf16[16,256,2,80]{1,3,2,0:T(8,128)(2,1)S(1)} fusion(bf16[16,256,2,80]{1,3,2,0:T(8,128)(2,1)S(1)} %get-tuple-element.126, s32[]{:T(128)} %get-tuple-element.125, bf16[4096,2,80]{0,2,1:T(8,128)(2,1)} %get-tuple-element.140, f32[2,256]{1,0:T(2,128)S(1)} %fusion.101, pred[256,4096]{1,0:T(8,128)(4,1)S(1)} %iota_compare_fusion.2, ...), kind=kOutput, calls=%fused_computation.14.clone.1 | convolution fusion | flops 681619968 | bytes 3836420 | tf_op jit(solution)/shard_map/while/body/eval_jaxpr/hqk,khd->qhd/dot_general | solution.py:54
  184.1 5.2 %fusion.102 = bf16[16,256,2,80]{1,3,2,0:T(8,128)(2,1)S(1)} fusion(bf16[16,256,2,80]{1,3,2,0:T(8,128)(2,1)S(1)} %get-tuple-element.126, s32[]{:T(128)} %get-tuple-element.125, bf16[4096,2,80]{0,2,1:T(8,128)(2,1)} %get-tuple-element.140, f32[2,256]{1,0:T(2,128)S(1)} %fusion.101, pred[256,4096]{1,0:T(8,128)(4,1)S(1)} %iota_compare_fusion.2, ...), kind=kOutput, calls=%fused_computation.14.clone.1 | convolution fusion | flops 681619968 | bytes 3836420 | tf_op jit(solution)/shard_map/while/body/eval_jaxpr/hqk,khd->qhd/dot_general | solution.py:54
  195.7 5.2 %fusion.102 = bf16[16,256,2,80]{1,3,2,0:T(8,128)(2,1)S(1)} fusion(bf16[16,256,2,80]{1,3,2,0:T(8,128)(2,1)S(1)} %get-tuple-element.126, s32[]{:T(128)} %get-tuple-element.125, bf16[4096,2,80]{0,2,1:T(8,128)(2,1)} %get-tuple-element.140, f32[2,256]{1,0:T(2,128)S(1)} %fusion.101, pred[256,4096]{1,0:T(8,128)(4,1)S(1)} %iota_compare_fusion.2, ...), kind=kOutput, calls=%fused_computation.14.clone.1 | convolution fusion | flops 681619968 | bytes 3836420 | tf_op jit(solution)/shard_map/while/body/eval_jaxpr/hqk,khd->qhd/dot_general | solution.py:54
  202.9 4.4 fusion.101
  207.4 5.2 %fusion.102 = bf16[16,256,2,80]{1,3,2,0:T(8,128)(2,1)S(1)} fusion(bf16[16,256,2,80]{1,3,2,0:T(8,128)(2,1)S(1)} %get-tuple-element.126, s32[]{:T(128)} %get-tuple-element.125, bf16[4096,2,80]{0,2,1:T(8,128)(2,1)} %get-tuple-element.140, f32[2,256]{1,0:T(2,128)S(1)} %fusion.101, pred[256,4096]{1,0:T(8,128)(4,1)S(1)} %iota_compare_fusion.2, ...), kind=kOutput, calls=%fused_computation.14.clone.1 | convolution fusion | flops 681619968 | bytes 3836420 | tf_op jit(solution)/shard_map/while/body/eval_jaxpr/hqk,khd->qhd/dot_general | solution.py:54
  219.0 5.2 %fusion.102 = bf16[16,256,2,80]{1,3,2,0:T(8,128)(2,1)S(1)} fusion(bf16[16,256,2,80]{1,3,2,0:T(8,128)(2,1)S(1)} %get-tuple-element.126, s32[]{:T(128)} %get-tuple-element.125, bf16[4096,2,80]{0,2,1:T(8,128)(2,1)} %get-tuple-element.140, f32[2,256]{1,0:T(2,128)S(1)} %fusion.101, pred[256,4096]{1,0:T(8,128)(4,1)S(1)} %iota_compare_fusion.2, ...), kind=kOutput, calls=%fused_computation.14.clone.1 | convolution fusion | flops 681619968 | bytes 3836420 | tf_op jit(solution)/shard_map/while/body/eval_jaxpr/hqk,khd->qhd/dot_general | solution.py:54
  230.7 5.2 %fusion.102 = bf16[16,256,2,80]{1,3,2,0:T(8,128)(2,1)S(1)} fusion(bf16[16,256,2,80]{1,3,2,0:T(8,128)(2,1)S(1)} %get-tuple-element.126, s32[]{:T(128)} %get-tuple-element.125, bf16[4096,2,80]{0,2,1:T(8,128)(2,1)} %get-tuple-element.140, f32[2,256]{1,0:T(2,128)S(1)} %fusion.101, pred[256,4096]{1,0:T(8,128)(4,1)S(1)} %iota_compare_fusion.2, ...), kind=kOutput, calls=%fused_computation.14.clone.1 | convolution fusion | flops 681619968 | bytes 3836420 | tf_op jit(solution)/shard_map/while/body/eval_jaxpr/hqk,khd->qhd/dot_general | solution.py:54
  242.3 5.2 %fusion.102 = bf16[16,256,2,80]{1,3,2,0:T(8,128)(2,1)S(1)} fusion(bf16[16,256,2,80]{1,3,2,0:T(8,128)(2,1)S(1)} %get-tuple-element.126, s32[]{:T(128)} %get-tuple-element.125, bf16[4096,2,80]{0,2,1:T(8,128)(2,1)} %get-tuple-element.140, f32[2,256]{1,0:T(2,128)S(1)} %fusion.101, pred[256,4096]{1,0:T(8,128)(4,1)S(1)} %iota_compare_fusion.2, ...), kind=kOutput, calls=%fused_computation.14.clone.1 | convolution fusion | flops 681619968 | bytes 3836420 | tf_op jit(solution)/shard_map/while/body/eval_jaxpr/hqk,khd->qhd/dot_general | solution.py:54
  254.0 5.2 %fusion.102 = bf16[16,256,2,80]{1,3,2,0:T(8,128)(2,1)S(1)} fusion(bf16[16,256,2,80]{1,3,2,0:T(8,128)(2,1)S(1)} %get-tuple-element.126, s32[]{:T(128)} %get-tuple-element.125, bf16[4096,2,80]{0,2,1:T(8,128)(2,1)} %get-tuple-element.140, f32[2,256]{1,0:T(2,128)S(1)} %fusion.101, pred[256,4096]{1,0:T(8,128)(4,1)S(1)} %iota_compare_fusion.2, ...), kind=kOutput, calls=%fused_computation.14.clone.1 | convolution fusion | flops 681619968 | bytes 3836420 | tf_op jit(solution)/shard_map/while/body/eval_jaxpr/hqk,khd->qhd/dot_general | solution.py:54
  265.6 5.2 %fusion.102 = bf16[16,256,2,80]{1,3,2,0:T(8,128)(2,1)S(1)} fusion(bf16[16,256,2,80]{1,3,2,0:T(8,128)(2,1)S(1)} %get-tuple-element.126, s32[]{:T(128)} %get-tuple-element.125, bf16[4096,2,80]{0,2,1:T(8,128)(2,1)} %get-tuple-element.140, f32[2,256]{1,0:T(2,128)S(1)} %fusion.101, pred[256,4096]{1,0:T(8,128)(4,1)S(1)} %iota_compare_fusion.2, ...), kind=kOutput, calls=%fused_computation.14.clone.1 | convolution fusion | flops 681619968 | bytes 3836420 | tf_op jit(solution)/shard_map/while/body/eval_jaxpr/hqk,khd->qhd/dot_general | solution.py:54
  272.8 4.4 fusion.101
  277.3 5.2 %fusion.102 = bf16[16,256,2,80]{1,3,2,0:T(8,128)(2,1)S(1)} fusion(bf16[16,256,2,80]{1,3,2,0:T(8,128)(2,1)S(1)} %get-tuple-element.126, s32[]{:T(128)} %get-tuple-element.125, bf16[4096,2,80]{0,2,1:T(8,128)(2,1)} %get-tuple-element.140, f32[2,256]{1,0:T(2,128)S(1)} %fusion.101, pred[256,4096]{1,0:T(8,128)(4,1)S(1)} %iota_compare_fusion.2, ...), kind=kOutput, calls=%fused_computation.14.clone.1 | convolution fusion | flops 681619968 | bytes 3836420 | tf_op jit(solution)/shard_map/while/body/eval_jaxpr/hqk,khd->qhd/dot_general | solution.py:54
  288.9 5.2 %fusion.102 = bf16[16,256,2,80]{1,3,2,0:T(8,128)(2,1)S(1)} fusion(bf16[16,256,2,80]{1,3,2,0:T(8,128)(2,1)S(1)} %get-tuple-element.126, s32[]{:T(128)} %get-tuple-element.125, bf16[4096,2,80]{0,2,1:T(8,128)(2,1)} %get-tuple-element.140, f32[2,256]{1,0:T(2,128)S(1)} %fusion.101, pred[256,4096]{1,0:T(8,128)(4,1)S(1)} %iota_compare_fusion.2, ...), kind=kOutput, calls=%fused_computation.14.clone.1 | convolution fusion | flops 681619968 | bytes 3836420 | tf_op jit(solution)/shard_map/while/body/eval_jaxpr/hqk,khd->qhd/dot_general | solution.py:54
  300.6 5.2 %fusion.102 = bf16[16,256,2,80]{1,3,2,0:T(8,128)(2,1)S(1)} fusion(bf16[16,256,2,80]{1,3,2,0:T(8,128)(2,1)S(1)} %get-tuple-element.126, s32[]{:T(128)} %get-tuple-element.125, bf16[4096,2,80]{0,2,1:T(8,128)(2,1)} %get-tuple-element.140, f32[2,256]{1,0:T(2,128)S(1)} %fusion.101, pred[256,4096]{1,0:T(8,128)(4,1)S(1)} %iota_compare_fusion.2, ...), kind=kOutput, calls=%fused_computation.14.clone.1 | convolution fusion | flops 681619968 | bytes 3836420 | tf_op jit(solution)/shard_map/while/body/eval_jaxpr/hqk,khd->qhd/dot_general | solution.py:54
  312.3 5.2 %fusion.102 = bf16[16,256,2,80]{1,3,2,0:T(8,128)(2,1)S(1)} fusion(bf16[16,256,2,80]{1,3,2,0:T(8,128)(2,1)S(1)} %get-tuple-element.126, s32[]{:T(128)} %get-tuple-element.125, bf16[4096,2,80]{0,2,1:T(8,128)(2,1)} %get-tuple-element.140, f32[2,256]{1,0:T(2,128)S(1)} %fusion.101, pred[256,4096]{1,0:T(8,128)(4,1)S(1)} %iota_compare_fusion.2, ...), kind=kOutput, calls=%fused_computation.14.clone.1 | convolution fusion | flops 681619968 | bytes 3836420 | tf_op jit(solution)/shard_map/while/body/eval_jaxpr/hqk,khd->qhd/dot_general | solution.py:54
  323.9 5.2 %fusion.102 = bf16[16,256,2,80]{1,3,2,0:T(8,128)(2,1)S(1)} fusion(bf16[16,256,2,80]{1,3,2,0:T(8,128)(2,1)S(1)} %get-tuple-element.126, s32[]{:T(128)} %get-tuple-element.125, bf16[4096,2,80]{0,2,1:T(8,128)(2,1)} %get-tuple-element.140, f32[2,256]{1,0:T(2,128)S(1)} %fusion.101, pred[256,4096]{1,0:T(8,128)(4,1)S(1)} %iota_compare_fusion.2, ...), kind=kOutput, calls=%fused_computation.14.clone.1 | convolution fusion | flops 681619968 | bytes 3836420 | tf_op jit(solution)/shard_map/while/body/eval_jaxpr/hqk,khd->qhd/dot_general | solution.py:54
  335.6 5.2 %fusion.102 = bf16[16,256,2,80]{1,3,2,0:T(8,128)(2,1)S(1)} fusion(bf16[16,256,2,80]{1,3,2,0:T(8,128)(2,1)S(1)} %get-tuple-element.126, s32[]{:T(128)} %get-tuple-element.125, bf16[4096,2,80]{0,2,1:T(8,128)(2,1)} %get-tuple-element.140, f32[2,256]{1,0:T(2,128)S(1)} %fusion.101, pred[256,4096]{1,0:T(8,128)(4,1)S(1)} %iota_compare_fusion.2, ...), kind=kOutput, calls=%fused_computation.14.clone.1 | convolution fusion | flops 681619968 | bytes 3836420 | tf_op jit(solution)/shard_map/while/body/eval_jaxpr/hqk,khd->qhd/dot_general | solution.py:54
  342.4 57.9 %all_to_all.33 = bf16[4096,2,80]{2,1,0:T(2,128)(2,1)} all-to-all(bf16[4096,2,80]{2,1,0:T(2,128)(2,1)S(1)} %bitcast.56), channel_id=1, replica_groups=mesh['data'=4,'seq'=16] {'seq'}, dimensions={0} | all-to-all | bytes 2621440 | tf_op jit(solution)/shard_map/all_to_all | solution.py:73
  400.2 4.6 copy.29
  404.9 8.5 %fusion.49 = (f32[256]{0:T(256)S(1)}, bf16[256,2560]{1,0:T(8,128)(2,1)S(1)}) fusion(bf16[256,2560]{0,1:T(8,128)(2,1)S(1)} %bitcast.58, bf16[2560,2560]{1,0:T(8,128)(2,1)} %bitcast.52, bf16[256,2560]{1,0:T(8,128)(2,1)S(1)} %copy-done), kind=kOutput, calls=%fused_computation.51 | convolution fusion | flops 3359375104 | bytes 17040384 | tf_op jit(solution)/shard_map/dot_general | solution.py:74
  414.5 25.2 %fusion.54 = f32[256,10240]{1,0:T(8,128)} fusion(bf16[2560,10240]{1,0:T(8,128)(2,1)} %param.15, bf16[256,2560]{1,0:T(8,128)(2,1)S(1)} %get-tuple-element.77, f32[2560]{0:T(1024)S(1)} %copy-done.4, f32[256]{0:T(256)S(1)} %add_rsqrt_fusion), kind=kOutput, calls=%fused_computation.56 | convolution fusion | flops 13424394240 | bytes 64236544 | tf_op jit(solution)/shard_map/dot_general | solution.py:30
  439.7 27.1 %fusion.34.clone.8 = bf16[256,10240]{1,0:T(8,128)(2,1)} fusion(bf16[2560,10240]{1,0:T(8,128)(2,1)} %param.16, f32[256,10240]{1,0:T(8,128)} %fusion.54, bf16[256,2560]{1,0:T(8,128)(2,1)} %copy-done.2, f32[2560]{0:T(1024)S(1)} %copy-done.4, f32[256]{0:T(256)S(1)} %add_rsqrt_fusion), kind=kOutput, calls=%fused_computation.28.clone.clone.clone.clone.clone.clone.clone.1 | convolution fusion | flops 13440122880 | bytes 69479424 | tf_op jit(solution)/shard_map/dot_general | solution.py:31
  466.7 24.4 %fusion.45 = bf16[256,2560]{1,0:T(8,128)(2,1)} fusion(bf16[10240,2560]{1,0:T(8,128)(2,1)} %param.17, bf16[256,2560]{1,0:T(8,128)(2,1)S(1)} %copy-done.3, bf16[256,10240]{1,0:T(8,128)(2,1)} %fusion.34.clone.8), kind=kOutput, calls=%fused_computation.47 | convolution fusion | flops 13423738880 | bytes 60293120 | tf_op jit(solution)/shard_map/dot_general | solution.py:33
  (86 shorter events, 96.3 us)
Async XLA Ops:
  32.6 3.8 copy-start.1
  38.9 97.9 %all-to-all-start = ((bf16[256,3,32,80]{0,3,1,2:T(8,128)(2,1)}), bf16[256,3,32,80]{0,3,1,2:T(8,128)(2,1)}, u32[]{:S(2)}, u32[]{:S(2)}) async-start(bf16[256,3,32,80]{0,3,1,2:T(8,128)(2,1)} %copy.20), calls=%async_computation | async-start | bytes 7864320 | tf_op jit(solution)/shard_map/all_to_all | solution.py:71
  400.2 4.7 copy-start
  404.9 9.6 %copy-start.4 = (f32[2560]{0:T(1024)S(1)}, f32[2560]{0:T(1024)}, u32[]{:S(2)}) copy-start(f32[2560]{0:T(1024)} %param.14) | copy-start | bytes 30724
  413.4 1.1 copy-start.2
  439.7 27.1 %copy-start.3 = (bf16[256,2560]{1,0:T(8,128)(2,1)S(1)}, bf16[256,2560]{1,0:T(8,128)(2,1)}, u32[]{:S(2)}) copy-start(bf16[256,2560]{1,0:T(8,128)(2,1)} %copy-done.2) | copy-start | bytes 3932164
where the time goes:
time: 493 us; the launch traced here: 491 us
  matrix products  263 us (53%)
  waiting for transfers between devices  87.2 us (18%)
  blocking collectives  57.9 us (12%)
  local copies, waits for them, and re-layouts  39.6 us (8%)
  other arithmetic  21.5 us (4%)
  loops' own time  10.9 us (2%)
  starting transfers between devices  10.7 us (2%)
    all_to_all x1, waiting for transfers between devices, local_layer(): head_major = lax.all_to_all(packed, 'seq', 2, 0, tiled=True)  87.2 us
    dot_general x16, matrix products, one_block(): jnp.einsum('hqk,khd->qhd', attn_probs, value_rows, preferred_element_type...  83.9 us
    sub x16, matrix products, one_block(): attn_probs = jax.nn.softmax(scores, axis=-1).astype(jnp.bfloat16)  71.1 us
    all_to_all x1, blocking collectives, local_layer(): attn_rows = lax.all_to_all(attn_heads, 'seq', 0, 1, tiled=True)  57.9 us
    dot_general x1, matrix products, gated_mlp(): up_pre = jnp.dot(y_norm, w_up, preferred_element_type=jnp.float32)  27.1 us
    dot_general x1, matrix products, gated_mlp(): gate_pre = jnp.dot(y_norm, w_gate, preferred_element_type=jnp.float32)  25.2 us
    dot_general x1, matrix products, gated_mlp(): jnp.dot(hidden, w_down, preferred_element_type=jnp.float32)  24.4 us
    dot_general x1, matrix products, local_layer(): jnp.dot(x_norm, w_qkv, preferred_element_type=jnp.float32)  23 us
  transfers between devices with their start and end apart: 1, of which 1 were waited for; matrix products, arithmetic and copies ran while one was open for 0% of the time, Pallas kernels for 0%

commit v1 on v0

v1 whole, which is shorter than its diff:
```python
import functools
import math

import jax
import jax.numpy as jnp
from jax import lax
from jax.experimental import pallas as pl
from jax.experimental.pallas import tpu as pltpu
from jax.sharding import PartitionSpec as P

ROPE_BASE = 10000
LOG2E = math.log2(math.e)


def rms_norm(row_vals, gain_vec):
    rows_f32 = row_vals.astype(jnp.float32)
    inv_rms = lax.rsqrt(jnp.mean(rows_f32 * rows_f32, axis=-1, keepdims=True) + 1e-5)
    return (rows_f32 * inv_rms * gain_vec).astype(jnp.bfloat16)


def rope_tables_t(positions, head_dim):
    inv_freq = 1.0 / (ROPE_BASE ** (jnp.arange(0, head_dim, 2, dtype=jnp.float32) / head_dim))
    angles = inv_freq[:, None] * positions.astype(jnp.float32)[None, :]
    return jnp.cos(angles), jnp.sin(angles)


def attention_kernel(n, hpd, hd, group, x_ref, g_ref, cos_ref, sin_ref, w_ref, o_ref,
                     wbuf, xn, sendb, recvb, kbuf, osend, orecv, wsem, ssem, rsem, osem, orsem):
    rows = x_ref.shape[0]
    inner = n * hpd * hd
    gcols = group * hpd * hd
    ngroups = n // group
    me = lax.axis_index('seq')
    mygrp = me // group

    def w_copy(g, t):
        grp = lax.rem(mygrp + ngroups // 2 + g, ngroups)
        col = pl.multiple_of(t * inner + grp * gcols, 128)
        return pltpu.make_async_copy(w_ref.at[:, pl.ds(col, gcols)], wbuf.at[t], wsem.at[t])

    for t in range(3):
        w_copy(0, t).start()

    barrier = pltpu.get_barrier_semaphore()

    def greet(k, c):
        pl.semaphore_signal(barrier, inc=1, device_id={'seq': lax.rem(me + k, n)}, device_id_type=pl.DeviceIdType.MESH)
        return c

    lax.fori_loop(1, n, greet, 0)
    xn[...] = rms_norm(x_ref[...], g_ref[...])
    pl.semaphore_wait(barrier, n - 1)

    def qkv_send(dest, h):
        return pltpu.make_async_remote_copy(
            src_ref=sendb.at[dest, h], dst_ref=recvb.at[me, h], send_sem=ssem.at[dest, h], recv_sem=rsem.at[me, h],
            device_id={'seq': dest}, device_id_type=pl.DeviceIdType.MESH)

    def qkv_recv(src, h):
        return pltpu.make_async_remote_copy(
            src_ref=sendb.at[src, h], dst_ref=recvb.at[src, h], send_sem=ssem.at[src, h], recv_sem=rsem.at[src, h],
            device_id={'seq': src}, device_id_type=pl.DeviceIdType.MESH)

    def qkv_local(h):
        return pltpu.make_async_copy(sendb.at[me, h], recvb.at[me, h], rsem.at[me, h])

    def project(g, c):
        grp = lax.rem(mygrp + ngroups // 2 + g, ngroups)
        for t in range(3):
            w_copy(g, t).wait()
            acc = jnp.dot(xn[...], wbuf[t], preferred_element_type=jnp.float32)

            @pl.when(g < ngroups - 1)
            def _():
                w_copy(g + 1, t).start()

            acc_t = acc.T
            for k in range(group * hpd):
                u = acc_t[k * hd:(k + 1) * hd]
                if t < 2:
                    lo, hi = u[:hd // 2], u[hd // 2:]
                    cos, sin = cos_ref[...], sin_ref[...]
                    u = jnp.concatenate([lo * cos - hi * sin, hi * cos + lo * sin], axis=0)
                sendb[grp * group + k // hpd, k % hpd, t * hd:(t + 1) * hd, :] = u.astype(jnp.bfloat16)

        def first_head(k, c):
            dest = grp * group + k

            @pl.when(dest != me)
            def _():
                qkv_send(dest, 0).start()
            return c

        lax.fori_loop(0, group, first_head, 0)
        return c

    lax.fori_loop(0, ngroups, project, 0)

    for h in range(hpd):
        qkv_local(h).start()

        if h > 0:
            def later_head(k, c):
                qkv_send(lax.rem(me + k, n), h).start()
                return c

            lax.fori_loop(1, n, later_head, 0)

    def o_send(dest, h):
        return pltpu.make_async_remote_copy(
            src_ref=osend.at[dest, h], dst_ref=orecv.at[me, h], send_sem=osem.at[dest, h], recv_sem=orsem.at[me, h],
            device_id={'seq': dest}, device_id_type=pl.DeviceIdType.MESH)

    def o_recv(src, h):
        return pltpu.make_async_remote_copy(
            src_ref=osend.at[src, h], dst_ref=orecv.at[src, h], send_sem=osem.at[src, h], recv_sem=orsem.at[src, h],
            device_id={'seq': src}, device_id_type=pl.DeviceIdType.MESH)

    def o_local(h):
        return pltpu.make_async_copy(osend.at[me, h], orecv.at[me, h], orsem.at[me, h])

    per = 2
    tile = per * rows
    scale2 = LOG2E * hd ** -0.5

    for h in range(hpd):
        def arrive(src, c):
            @pl.when(src != me)
            def _():
                qkv_recv(src, h).wait_recv()

            @pl.when(src == me)
            def _():
                qkv_local(h).wait()

            kbuf[pl.ds(pl.multiple_of(src * rows, rows), rows), :] = recvb[src, h, hd:2 * hd, :].T
            return c

        lax.fori_loop(0, n, arrive, 0)

        def q_tile(i, c):
            q_t = jnp.concatenate([recvb[per * i + r, h, 0:hd, :] for r in range(per)], axis=1)

            def scores(j):
                k_blk = kbuf[pl.ds(pl.multiple_of(j * tile, tile), tile), :]
                return jnp.dot(k_blk, q_t, preferred_element_type=jnp.float32)

            def values(j):
                return jnp.concatenate([recvb[per * j + r, h, 2 * hd:3 * hd, :] for r in range(per)], axis=1)

            s = scores(i)
            key_pos = lax.broadcasted_iota(jnp.int32, s.shape, 0)
            query_pos = lax.broadcasted_iota(jnp.int32, s.shape, 1)
            s = jnp.where(key_pos <= query_pos, s, -jnp.inf)
            m = jnp.max(s, axis=0, keepdims=True)
            p = jnp.exp2((s - m) * scale2)
            l = jnp.sum(p, axis=0, keepdims=True)
            acc = jnp.dot(values(i), p.astype(jnp.bfloat16), preferred_element_type=jnp.float32)

            def kv_tile(j, carry):
                m, l, acc = carry
                s = scores(j)
                m_new = jnp.maximum(m, jnp.max(s, axis=0, keepdims=True))
                p = jnp.exp2((s - m_new) * scale2)
                alpha = jnp.exp2((m - m_new) * scale2)
                l = alpha * l + jnp.sum(p, axis=0, keepdims=True)
                acc = alpha * acc + jnp.dot(values(j), p.astype(jnp.bfloat16), preferred_element_type=jnp.float32)
                return m_new, l, acc

            m, l, acc = lax.fori_loop(0, i, kv_tile, (m, l, acc))
            out = (acc / l).astype(jnp.bfloat16)
            for r in range(per):
                dest = per * i + r
                osend[dest, h] = out[:, r * rows:(r + 1) * rows]

                @pl.when(dest != me)
                def _():
                    o_send(dest, h).start()

                @pl.when(dest == me)
                def _():
                    o_local(h).start()
            return c

        lax.fori_loop(0, n // per, q_tile, 0)

    def finish(k, c):
        other = lax.rem(me + k, n)
        for h in range(hpd):
            o_recv(other, h).wait_recv()
            qkv_send(other, h).wait_send()
            o_send(other, h).wait_send()
        return c

    lax.fori_loop(1, n, finish, 0)
    for h in range(hpd):
        o_local(h).wait()
    o_ref[...] = orecv[...]


def attention_rows(x_blk, g_attn, w_qkv, cos_t, sin_t, n, n_heads, head_dim):
    rows, width = x_blk.shape
    hpd = n_heads // n
    group = 1
    while (group * hpd * head_dim) % 128:
        group *= 2
    gcols = group * hpd * head_dim
    vmem = pl.BlockSpec(memory_space=pltpu.VMEM)
    kernel = functools.partial(attention_kernel, n, hpd, head_dim, group)
    bf16 = jnp.bfloat16
    return pl.pallas_call(
        kernel,
        out_shape=jax.ShapeDtypeStruct((n, hpd, head_dim, rows), bf16),
        in_specs=[vmem, vmem, vmem, vmem, pl.BlockSpec(memory_space=pl.ANY)],
        out_specs=vmem,
        scratch_shapes=[
            pltpu.VMEM((3, width, gcols), bf16),
            pltpu.VMEM((rows, width), bf16),
            pltpu.VMEM((n, hpd, 3 * head_dim, rows), bf16),
            pltpu.VMEM((n, hpd, 3 * head_dim, rows), bf16),
            pltpu.VMEM((n * rows, head_dim), bf16),
            pltpu.VMEM((n, hpd, head_dim, rows), bf16),
            pltpu.VMEM((n, hpd, head_dim, rows), bf16),
            pltpu.SemaphoreType.DMA((3,)),
            pltpu.SemaphoreType.DMA((n, hpd)),
            pltpu.SemaphoreType.DMA((n, hpd)),
            pltpu.SemaphoreType.DMA((n, hpd)),
            pltpu.SemaphoreType.DMA((n, hpd)),
        ],
        compiler_params=pltpu.CompilerParams(collective_id=0, has_side_effects=True, vmem_limit_bytes=60 * 1024 * 1024),
        name='attention',
    )(x_blk, g_attn, cos_t, sin_t, w_qkv)


def gated_mlp(y_rows, g_mlp, w_gate, w_up, w_down):
    y_norm = rms_norm(y_rows, g_mlp)
    gate_pre = jnp.dot(y_norm, w_gate, preferred_element_type=jnp.float32)
    up_pre = jnp.dot(y_norm, w_up, preferred_element_type=jnp.float32)
    hidden = (jax.nn.silu(gate_pre) * up_pre).astype(jnp.bfloat16)
    return (y_rows.astype(jnp.float32) + jnp.dot(hidden, w_down, preferred_element_type=jnp.float32)).astype(jnp.bfloat16)


def solution(mesh):
    n = mesh.shape['seq']

    def local_layer(x_blk, g_attn, w_qkv, w_out, g_mlp, w_gate, w_up, w_down):
        n_heads, head_dim, model_width = w_out.shape
        local_rows = x_blk.shape[0]
        member = lax.axis_index('seq')
        positions = member * local_rows + jnp.arange(local_rows)
        cos_t, sin_t = rope_tables_t(positions, head_dim)
        o_t = attention_rows(x_blk, g_attn[None, :], w_qkv, cos_t, sin_t, n, n_heads, head_dim)
        o_t = o_t.reshape(n_heads * head_dim, local_rows)
        attn_mixed = lax.dot_general(o_t, w_out.reshape(n_heads * head_dim, model_width), (((0,), (0,)), ((), ())),
                                     preferred_element_type=jnp.float32)
        y_rows = (x_blk.astype(jnp.float32) + attn_mixed).astype(jnp.bfloat16)
        return gated_mlp(y_rows, g_mlp, w_gate, w_up, w_down)

    row_spec = P(('data', 'seq'), None)
    return jax.shard_map(local_layer, mesh=mesh, in_specs=(row_spec, P(), P(), P(), P(), P(), P(), P()), out_specs=row_spec, check_vma=False)
```

time: 493 us -> 222 us (0.45)
  matrix products: 263 us -> 84.9 us
  Pallas kernels: 0 us -> 135 us
  waiting for transfers between devices: 87.2 us -> 0 us
  blocking collectives: 57.9 us -> 0 us
  local copies, waits for them, and re-layouts: 39.6 us -> 1.32 us
  other arithmetic: 21.5 us -> 0.87 us
  loops' own time: 10.9 us -> 0 us
  starting transfers between devices: 10.7 us -> 0 us
    pallas_call x0 -> x1, Pallas kernels: none -> 135 us  [attention_rows(): pl.pallas_call(kernel, out_shape=jax.ShapeDtypeStruct((n, hpd, head_dim,...]
    dot_general x18 -> x1, matrix products: 115 us -> 8.93 us  [local_layer(): lax.dot_general(o_t, w_out.reshape(n_heads * head_dim, model_width), (((0...]
    all_to_all x1 -> x0, waiting for transfers between devices: 87.2 us -> none  [local_layer(): head_major = lax.all_to_all(packed, 'seq', 2, 0, tiled=True)]
    sub x16 -> x0, matrix products: 71.1 us -> none  [one_block(): attn_probs = jax.nn.softmax(scores, axis=-1).astype(jnp.bfloat16)]
    all_to_all x1 -> x0, blocking collectives: 57.9 us -> none  [local_layer(): attn_rows = lax.all_to_all(attn_heads, 'seq', 0, 1, tiled=True)]
    all_to_all x3 -> x0, local copies, waits for them, and re-layouts: 18 us -> none  [the longest x2 13.3 us: local_layer(): head_major = lax.all_to_all(packed, 'seq', 2, 0, tiled=True)]
    another operation x1 -> x0, loops' own time: 10.9 us -> none  [causal_attention(): blocks = lax.map(one_block, jnp.arange(total_rows // block_rows))]
    all_to_all x1 -> x0, starting transfers between devices: 10.7 us -> none  [local_layer(): head_major = lax.all_to_all(packed, 'seq', 2, 0, tiled=True)]
  transfers between devices with their start and end apart: 1 -> 0, of which waited for: 1 -> 0; matrix products, arithmetic and copies ran while one was open for 0% -> 0% of each run, Pallas kernels for 0% -> 0%
where the time goes in v1:
time: 222 us
  Pallas kernels  135 us (61%)
  matrix products  84.9 us (38%)
    pallas_call x1, Pallas kernels, attention_rows(): pl.pallas_call(kernel, out_shape=jax.ShapeDtypeStruct((n, hpd, head_dim,...  135 us
    dot_general x1, matrix products, gated_mlp(): up_pre = jnp.dot(y_norm, w_up, preferred_element_type=jnp.float32)  26.6 us
    dot_general x1, matrix products, gated_mlp(): gate_pre = jnp.dot(y_norm, w_gate, preferred_element_type=jnp.float32)  25.2 us
    dot_general x1, matrix products, gated_mlp(): jnp.dot(hidden, w_down, preferred_element_type=jnp.float32)  24.1 us
    dot_general x1, matrix products, local_layer(): lax.dot_general(o_t, w_out.reshape(n_heads * head_dim, model_width), (((0...  8.93 us

profile of v1, /device:TPU:21, one launch (start us, length us, event | category | flops | bytes accessed | tf_op | source)
XLA Modules:
  0.0 222.1 jit_solution(6592823741577412232)
XLA Ops:
  0.0 1.3 broadcast_in_dim.2.g_ref
  1.3 0.8 multiply_sine_fusion
  2.2 0.0 copy-start
  2.2 135.0 %attention.1 = bf16[16,2,80,256]{3,2,1,0:T(8,128)(2,1)} custom-call(bf16[256,2560]{1,0:T(8,128)(2,1)} %x_ref.1, f32[1,2560]{1,0:T(1,128)} %broadcast_in_dim.2.g_ref, f32[40,256]{1,0:T(8,128)} %get-tuple-element.6.cos_ref, f32[40,256]{1,0:T(8,128)} %get-tuple-element.5.sin_ref, bf16[2560,7680]{1,0:T(8,128)(2,1)} %w_ref.1), custom_call_target="tpu_custom_call" | custom-call | tf_op jit(solution)/shard_map/attention/pallas_call | solution.py:211
  137.2 0.0 copy-done
  137.2 0.0 copy-start.1
  137.2 8.9 %fusion.10 = (f32[256]{0:T(256)S(1)}, bf16[256,2560]{1,0:T(8,128)(2,1)S(1)}) fusion(bf16[2560,256]{1,0:T(8,128)(2,1)} %bitcast.13, bf16[2560,2560]{1,0:T(8,128)(2,1)} %bitcast.12, bf16[256,2560]{1,0:T(8,128)(2,1)S(1)} %copy-done), kind=kOutput, calls=%fused_computation.14 | convolution fusion | flops 3359375104 | bytes 17040384 | tf_op jit(solution)/shard_map/dot_general | solution.py:254
  146.1 0.0 copy-done.1
  146.1 25.2 %fusion.15 = f32[256,10240]{1,0:T(8,128)} fusion(bf16[2560,10240]{1,0:T(8,128)(2,1)} %param.13, bf16[256,2560]{1,0:T(8,128)(2,1)S(1)} %get-tuple-element.8, f32[2560]{0:T(1024)S(1)} %copy-done.1, f32[256]{0:T(256)S(1)} %add_rsqrt_fusion), kind=kOutput, calls=%fused_computation.17 | convolution fusion | flops 13424394240 | bytes 64236544 | tf_op jit(solution)/shard_map/dot_general | solution.py:237
  171.4 26.6 %fusion.clone.8 = bf16[256,10240]{1,0:T(8,128)(2,1)} fusion(bf16[2560,10240]{1,0:T(8,128)(2,1)} %param.14, f32[256,10240]{1,0:T(8,128)} %fusion.15, bf16[256,2560]{1,0:T(8,128)(2,1)S(1)} %get-tuple-element.8, f32[2560]{0:T(1024)S(1)} %copy-done.1, f32[256]{0:T(256)S(1)} %add_rsqrt_fusion), kind=kOutput, calls=%fused_computation.1.clone.clone.clone.clone.clone.clone.clone.1 | convolution fusion | flops 13440122880 | bytes 69479424 | tf_op jit(solution)/shard_map/dot_general | solution.py:238
  198.0 24.1 %fusion.9 = bf16[256,2560]{1,0:T(8,128)(2,1)} fusion(bf16[10240,2560]{1,0:T(8,128)(2,1)} %param.15, bf16[256,2560]{1,0:T(8,128)(2,1)S(1)} %get-tuple-element.8, bf16[256,10240]{1,0:T(8,128)(2,1)} %fusion.clone.8), kind=kOutput, calls=%fused_computation.13 | convolution fusion | flops 13423738880 | bytes 60293120 | tf_op jit(solution)/shard_map/dot_general | solution.py:240
  (3 shorter events, 0.0 us)
Async XLA Ops:
  2.2 135.0 %copy-start = (bf16[256,2560]{1,0:T(8,128)(2,1)S(1)}, bf16[256,2560]{1,0:T(8,128)(2,1)}, u32[]{:S(2)}) copy-start(bf16[256,2560]{1,0:T(8,128)(2,1)} %x_ref.1) | copy-start | bytes 3932164
  137.2 9.0 %copy-start.1 = (f32[2560]{0:T(1024)S(1)}, f32[2560]{0:T(1024)}, u32[]{:S(2)}) copy-start(f32[2560]{0:T(1024)} %param.12) | copy-start | bytes 30724

commit v2 on v0

v2 whole, which is shorter than its diff:
```python
import functools
import math

import jax
import jax.numpy as jnp
from jax import lax
from jax.experimental import pallas as pl
from jax.experimental.pallas import tpu as pltpu
from jax.sharding import PartitionSpec as P

ROPE_BASE = 10000
LOG2E = math.log2(math.e)
HALVES = 2
MESH = pl.DeviceIdType.MESH


def rms_norm(row_vals, gain_vec):
    rows_f32 = row_vals.astype(jnp.float32)
    inv_rms = lax.rsqrt(jnp.mean(rows_f32 * rows_f32, axis=-1, keepdims=True) + 1e-5)
    return (rows_f32 * inv_rms * gain_vec).astype(jnp.bfloat16)


def rope_tables_t(positions, head_dim):
    inv_freq = 1.0 / (ROPE_BASE ** (jnp.arange(0, head_dim, 2, dtype=jnp.float32) / head_dim))
    angles = inv_freq[:, None] * positions.astype(jnp.float32)[None, :]
    return jnp.cos(angles), jnp.sin(angles)


def layer_kernel(n, hpd, hd, group, chunk, slots,
                 x_ref, ga_ref, gm_ref, cos_ref, sin_ref, wqkv_ref, wout_ref, wg_ref, wu_ref, wd_ref, z_ref,
                 wout, xn, kvs, kvr, qs, qr, kbuf, osend, orecv, yn, ybuf, acc, zrecv, wg, wu, wd,
                 stage_sem, wout_sem, w_sem, kv_ss, kv_rs, q_ss, q_rs, o_ss, o_rs, y_ss, y_rs, z_ss, z_rs):
    rows, width = x_ref.shape
    half_rows = rows // HALVES
    inner = n * hpd * hd
    gcols = group * hpd * hd
    ngroups = n // group
    stages = width // gcols
    ff_half = wg_ref.shape[1] // 2
    nchunks = ff_half // chunk
    me = lax.axis_index('seq')
    core = lax.rem(me, 2)
    partner = me + 1 - 2 * core
    mygrp = me // group

    def grp_of(g):
        return lax.rem(mygrp + ngroups // 2 + g, ngroups)

    def tile_copy(s, t, g):
        col = pl.multiple_of(t * inner + grp_of(g) * gcols, 128)
        slot = pl.multiple_of(lax.rem(s, stages) * gcols, 128)
        return pltpu.make_async_copy(wqkv_ref.at[:, pl.ds(col, gcols)], wout.at[:, pl.ds(slot, gcols)],
                                     stage_sem.at[lax.rem(s, stages)])

    def start_tile(s):
        @pl.when(s < 2 * ngroups)
        def _():
            tile_copy(s, 1 + lax.rem(s, 2), s // 2).start()

        @pl.when(jnp.logical_and(s >= 2 * ngroups, s < 3 * ngroups))
        def _():
            tile_copy(s, 0, s - 2 * ngroups).start()

    def chunk_copies(s):
        slot = lax.rem(s, slots)
        ff = pl.multiple_of(core * ff_half + lax.rem(s, nchunks) * chunk, 128)
        return (pltpu.make_async_copy(wg_ref.at[:, pl.ds(ff, chunk)], wg.at[slot], w_sem.at[0, slot]),
                pltpu.make_async_copy(wu_ref.at[:, pl.ds(ff, chunk)], wu.at[slot], w_sem.at[1, slot]),
                pltpu.make_async_copy(wd_ref.at[pl.ds(ff, chunk), :], wd.at[slot], w_sem.at[2, slot]))

    for s in range(stages):
        start_tile(s)

    barrier = pltpu.get_barrier_semaphore()

    def greet(k, c):
        pl.semaphore_signal(barrier, inc=1, device_id={'seq': lax.rem(me + k, n)}, device_id_type=MESH)
        return c

    lax.fori_loop(1, n, greet, 0)
    xn[...] = rms_norm(x_ref[...], ga_ref[...])
    pl.semaphore_wait(barrier, n - 1)

    def remote(src, dst, ssem, rsem, dest):
        return pltpu.make_async_remote_copy(src_ref=src, dst_ref=dst, send_sem=ssem, recv_sem=rsem,
                                            device_id={'seq': dest}, device_id_type=MESH)

    def kv_send(dest, h):
        return remote(kvs.at[dest, h], kvr.at[me, h], kv_ss.at[dest, h], kv_rs.at[me, h], dest)

    def kv_recv(src, h):
        return remote(kvs.at[src, h], kvr.at[src, h], kv_ss.at[src, h], kv_rs.at[src, h], src)

    def kv_local(h):
        return pltpu.make_async_copy(kvs.at[me, h], kvr.at[me, h], kv_rs.at[me, h])

    def q_send(dest, u):
        src, dst = (qs.at[dest, 0], qr.at[me, 0]) if u == 0 else (qs.at[dest, 1, u - 1], qr.at[me, 1, u - 1])
        return remote(src, dst, q_ss.at[dest, u], q_rs.at[me, u], dest)

    def q_recv(src, u):
        a, b = (qs.at[src, 0], qr.at[src, 0]) if u == 0 else (qs.at[src, 1, u - 1], qr.at[src, 1, u - 1])
        return remote(a, b, q_ss.at[src, u], q_rs.at[src, u], src)

    def q_local(u):
        src, dst = (qs.at[me, 0], qr.at[me, 0]) if u == 0 else (qs.at[me, 1, u - 1], qr.at[me, 1, u - 1])
        return pltpu.make_async_copy(src, dst, q_rs.at[me, u])

    def o_send(dest, f):
        return remote(osend.at[f, dest], orecv.at[f, me], o_ss.at[f, dest], o_rs.at[f, me], dest)

    def o_recv(src, f):
        return remote(osend.at[f, src], orecv.at[f, src], o_ss.at[f, src], o_rs.at[f, src], src)

    def o_local(f):
        return pltpu.make_async_copy(osend.at[f, me], orecv.at[f, me], o_rs.at[f, me])

    def project(s):
        start = pl.multiple_of(lax.rem(s, stages) * gcols, 128)
        out = jnp.dot(xn[...], wout[:, pl.ds(start, gcols)], preferred_element_type=jnp.float32)
        start_tile(s + stages)
        return out.T

    def rope(u):
        lo, hi = u[:hd // 2], u[hd // 2:]
        cos, sin = cos_ref[...], sin_ref[...]
        return jnp.concatenate([lo * cos - hi * sin, hi * cos + lo * sin], axis=0)

    def send_group(g, make):
        def one(k, c):
            dest = grp_of(g) * group + k

            @pl.when(dest != me)
            def _():
                make(dest).start()
            return c

        lax.fori_loop(0, group, one, 0)

    def project_kv(g, c):
        for t in (0, 1):
            tile_copy(2 * g + t, 1 + t, g).wait()
            out = project(2 * g + t)
            for k in range(group * hpd):
                u = out[k * hd:(k + 1) * hd]
                if t == 0:
                    u = rope(u)
                kvs[grp_of(g) * group + k // hpd, k % hpd, t * hd:(t + 1) * hd, :] = u.astype(jnp.bfloat16)
        send_group(g, lambda dest: kv_send(dest, 0))
        return c

    lax.fori_loop(0, ngroups, project_kv, 0)
    kv_local(0).start()
    kv_local(1).start()

    def project_q(g, c):
        s = 2 * ngroups + g
        tile_copy(s, 0, g).wait()
        out = project(s)
        for k in range(group * hpd):
            u = rope(out[k * hd:(k + 1) * hd]).astype(jnp.bfloat16)
            for f in range(HALVES):
                qs[grp_of(g) * group + k // hpd, k % hpd, f] = u[:, f * half_rows:(f + 1) * half_rows]
        send_group(g, lambda dest: q_send(dest, 0))
        return c

    lax.fori_loop(0, ngroups, project_q, 0)
    for u in range(3):
        q_local(u).start()

    def to_others(make):
        def one(k, c):
            make(lax.rem(me + k, n)).start()
            return c

        lax.fori_loop(1, n, one, 0)

    to_others(lambda dest: kv_send(dest, 1))

    wout_copy = pltpu.make_async_copy(wout_ref, wout, wout_sem)
    wout_copy.start()
    for s in range(slots):
        for copy in chunk_copies(s):
            copy.start()

    per = 4
    kv_per = 2
    q_tile = per * half_rows
    kv_tile = kv_per * rows
    scale2 = LOG2E * hd ** -0.5

    def arrive_kv(h):
        def one(src, c):
            @pl.when(src != me)
            def _():
                kv_recv(src, h).wait_recv()

            @pl.when(src == me)
            def _():
                kv_local(h).wait()

            kbuf[pl.ds(pl.multiple_of(src * rows, rows), rows), :] = kvr[src, h, 0:hd, :].T
            return c

        lax.fori_loop(0, n, one, 0)

    def arrive_q(u):
        def one(k, c):
            q_recv(lax.rem(me + k, n), u).wait_recv()
            return c

        lax.fori_loop(1, n, one, 0)
        q_local(u).wait()

    def attend(h, f):
        def one_tile(i, c):
            q_t = jnp.concatenate([qr[per * i + r, h, f] for r in range(per)], axis=1)

            def scores(j, q):
                k_blk = kbuf[pl.ds(pl.multiple_of(j * kv_tile, kv_tile), kv_tile), :]
                return jnp.dot(k_blk, q, preferred_element_type=jnp.float32)

            def values(j):
                return jnp.concatenate([kvr[kv_per * j + r, h, hd:2 * hd, :] for r in range(kv_per)], axis=1)

            def update(j, s, carry):
                m_new = jnp.max(s, axis=0, keepdims=True)
                if carry is not None:
                    m, l, o = carry
                    m_new = jnp.maximum(m, m_new)
                p = jnp.exp2((s - m_new) * scale2)
                l_new = jnp.sum(p, axis=0, keepdims=True)
                o_new = jnp.dot(values(j), p.astype(jnp.bfloat16), preferred_element_type=jnp.float32)
                if carry is not None:
                    alpha = jnp.exp2((m - m_new) * scale2)
                    l_new = alpha * l + l_new
                    o_new = alpha * o + o_new
                return m_new, l_new, o_new

            def masked(j, off, lane0):
                q = q_t[:, lane0:]
                s = scores(j, q)
                lane = lane0 + lax.broadcasted_iota(jnp.int32, s.shape, 1)
                query_pos = (lane // half_rows) * rows + f * half_rows + lane % half_rows
                key_pos = off + lax.broadcasted_iota(jnp.int32, s.shape, 0)
                return jnp.where(key_pos <= query_pos, s, -jnp.inf)

            diag = per // kv_per
            carry = update(diag * i, masked(diag * i, 0, 0), None)
            cut = q_tile // diag
            late = update(diag * i + 1, masked(diag * i + 1, kv_tile, cut), tuple(v[:, cut:] for v in carry))
            carry = tuple(jnp.concatenate([v[:, :cut], w], axis=1) for v, w in zip(carry, late))
            m, l, o = lax.fori_loop(0, diag * i, lambda j, cr: update(j, scores(j, q_t), cr), carry)
            out = (o / l).astype(jnp.bfloat16)
            for r in range(per):
                dest = per * i + r
                osend[f, dest, h] = out[:, r * half_rows:(r + 1) * half_rows]
                if h == hpd - 1:
                    @pl.when(dest != me)
                    def _():
                        o_send(dest, f).start()

                    @pl.when(dest == me)
                    def _():
                        o_local(f).start()
            return c

        lax.fori_loop(0, n // per, one_tile, 0)

    arrive_q(0)
    to_others(lambda dest: q_send(dest, 1))
    to_others(lambda dest: q_send(dest, 2))
    arrive_kv(0)
    attend(0, 0)
    attend(0, 1)
    arrive_kv(1)
    arrive_q(1)
    attend(1, 0)
    arrive_q(2)
    attend(1, 1)
    wout_copy.wait()

    def y_send(f):
        return remote(yn.at[f, 0], yn.at[f, 1], y_ss.at[f], y_rs.at[f], partner)

    def z_send(f):
        return remote(acc.at[f, 1], zrecv.at[f], z_ss.at[f], z_rs.at[f], partner)

    for f in range(HALVES):
        r0 = f * half_rows

        def arrive_o(k, c):
            o_recv(lax.rem(me + k, n), f).wait_recv()
            return c

        lax.fori_loop(1, n, arrive_o, 0)
        o_local(f).wait()
        o_rows = orecv[f].reshape(inner, half_rows).T
        mixed = jnp.dot(o_rows, wout[...], preferred_element_type=jnp.float32)
        y = (x_ref[r0:r0 + half_rows, :].astype(jnp.float32) + mixed).astype(jnp.bfloat16)
        ybuf[r0:r0 + half_rows, :] = y
        yn[f, 0] = rms_norm(y, gm_ref[...])
        y_send(f).start()
        acc[f] = jnp.zeros_like(acc[f])
        y_send(f).wait()

        def one_chunk(c, carry):
            s = f * nchunks + c
            slot = lax.rem(s, slots)
            cg, cu, cd = chunk_copies(s)
            y_all = yn[f].reshape(2 * half_rows, width)
            cg.wait()
            gate = jnp.dot(y_all, wg[slot], preferred_element_type=jnp.float32)
            cu.wait()
            up = jnp.dot(y_all, wu[slot], preferred_element_type=jnp.float32)
            hidden = (gate / (1.0 + jnp.exp(-gate)) * up).astype(jnp.bfloat16)
            cd.wait()
            part = jnp.dot(hidden, wd[slot], preferred_element_type=jnp.float32)
            acc[f] += part.reshape(2, half_rows, width)

            @pl.when(s + slots < HALVES * nchunks)
            def _():
                for copy in chunk_copies(s + slots):
                    copy.start()
            return carry

        lax.fori_loop(0, nchunks, one_chunk, 0)
        z_send(f).start()

    for f in range(HALVES):
        r0 = f * half_rows
        z_send(f).wait()
        total = acc[f, 0] + zrecv[f]
        z_ref[r0:r0 + half_rows, :] = (ybuf[r0:r0 + half_rows, :].astype(jnp.float32) + total).astype(jnp.bfloat16)

    def drain(k, c):
        other = lax.rem(me + k, n)
        for h in range(hpd):
            kv_send(other, h).wait_send()
        for u in range(3):
            q_send(other, u).wait_send()
        for f in range(HALVES):
            o_send(other, f).wait_send()
        return c

    lax.fori_loop(1, n, drain, 0)


def solution(mesh):
    n = mesh.shape['seq']

    def local_layer(x_blk, g_attn, w_qkv, w_out, g_mlp, w_gate, w_up, w_down):
        n_heads, hd, width = w_out.shape
        rows = x_blk.shape[0]
        hpd = n_heads // n
        member = lax.axis_index('seq')
        cos_t, sin_t = rope_tables_t(member * rows + jnp.arange(rows), hd)
        group = 1
        while (group * hpd * hd) % 128:
            group *= 2
        chunk, slots = 512, 2
        half = rows // HALVES
        bf16, f32 = jnp.bfloat16, jnp.float32
        vmem = pl.BlockSpec(memory_space=pltpu.VMEM)
        hbm = pl.BlockSpec(memory_space=pl.ANY)
        dma = pltpu.SemaphoreType.DMA
        return pl.pallas_call(
            functools.partial(layer_kernel, n, hpd, hd, group, chunk, slots),
            out_shape=jax.ShapeDtypeStruct(x_blk.shape, bf16),
            in_specs=[vmem] * 5 + [hbm] * 5,
            out_specs=vmem,
            scratch_shapes=[
                pltpu.VMEM((n_heads * hd, width), bf16),
                pltpu.VMEM((rows, width), bf16),
                pltpu.VMEM((n, hpd, 2 * hd, rows), bf16),
                pltpu.VMEM((n, hpd, 2 * hd, rows), bf16),
                pltpu.VMEM((n, hpd, HALVES, hd, half), bf16),
                pltpu.VMEM((n, hpd, HALVES, hd, half), bf16),
                pltpu.VMEM((n * rows, hd), bf16),
                pltpu.VMEM((HALVES, n, hpd, hd, half), bf16),
                pltpu.VMEM((HALVES, n, hpd, hd, half), bf16),
                pltpu.VMEM((HALVES, 2, half, width), bf16),
                pltpu.VMEM((rows, width), bf16),
                pltpu.VMEM((HALVES, 2, half, width), f32),
                pltpu.VMEM((HALVES, half, width), f32),
                pltpu.VMEM((slots, width, chunk), bf16),
                pltpu.VMEM((slots, width, chunk), bf16),
                pltpu.VMEM((slots, chunk, width), bf16),
                dma((4,)), dma, dma((3, slots)),
                dma((n, hpd)), dma((n, hpd)), dma((n, 3)), dma((n, 3)), dma((HALVES, n)), dma((HALVES, n)),
                dma((HALVES,)), dma((HALVES,)), dma((HALVES,)), dma((HALVES,)),
            ],
            compiler_params=pltpu.CompilerParams(collective_id=0, has_side_effects=True, vmem_limit_bytes=67043328),
            name='layer',
        )(x_blk, g_attn[None, :], g_mlp[None, :], cos_t, sin_t, w_qkv, w_out.reshape(n_heads * hd, width), w_gate, w_up, w_down)

    row_spec = P(('data', 'seq'), None)
    return jax.shard_map(local_layer, mesh=mesh, in_specs=(row_spec, P(), P(), P(), P(), P(), P(), P()), out_specs=row_spec, check_vma=False)
```

time: 493 us -> 194 us (0.39)
  matrix products: 263 us -> 0 us
  Pallas kernels: 0 us -> 188 us
  waiting for transfers between devices: 87.2 us -> 0 us
  blocking collectives: 57.9 us -> 0 us
  local copies, waits for them, and re-layouts: 39.6 us -> 5.08 us
  other arithmetic: 21.5 us -> 0.86 us
  loops' own time: 10.9 us -> 0 us
  starting transfers between devices: 10.7 us -> 0 us
    dot_general x21 -> x0, matrix products: 192 us -> none  [the longest x16 83.9 us: one_block(): jnp.einsum('hqk,khd->qhd', attn_probs, value_rows, preferred_element_type...]
    pallas_call x0 -> x1, Pallas kernels: none -> 188 us  [local_layer(): pl.pallas_call(functools.partial(layer_kernel, n, hpd, hd, group, chunk,...]
    all_to_all x1 -> x0, waiting for transfers between devices: 87.2 us -> none  [local_layer(): head_major = lax.all_to_all(packed, 'seq', 2, 0, tiled=True)]
    sub x16 -> x0, matrix products: 71.1 us -> none  [one_block(): attn_probs = jax.nn.softmax(scores, axis=-1).astype(jnp.bfloat16)]
    all_to_all x1 -> x0, blocking collectives: 57.9 us -> none  [local_layer(): attn_rows = lax.all_to_all(attn_heads, 'seq', 0, 1, tiled=True)]
    all_to_all x3 -> x0, local copies, waits for them, and re-layouts: 18 us -> none  [the longest x2 13.3 us: local_layer(): head_major = lax.all_to_all(packed, 'seq', 2, 0, tiled=True)]
    another operation x1 -> x0, loops' own time: 10.9 us -> none  [causal_attention(): blocks = lax.map(one_block, jnp.arange(total_rows // block_rows))]
    all_to_all x1 -> x0, starting transfers between devices: 10.7 us -> none  [local_layer(): head_major = lax.all_to_all(packed, 'seq', 2, 0, tiled=True)]
  transfers between devices with their start and end apart: 1 -> 0, of which waited for: 1 -> 0; matrix products, arithmetic and copies ran while one was open for 0% -> 0% of each run, Pallas kernels for 0% -> 0%
where the time goes in v2:
time: 194 us
  Pallas kernels  188 us (97%)
  local copies, waits for them, and re-layouts  5.08 us (3%)
    pallas_call x1, Pallas kernels, local_layer(): pl.pallas_call(functools.partial(layer_kernel, n, hpd, hd, group, chunk,...  188 us

profile of v2, /device:TPU:21, one launch (start us, length us, event | category | flops | bytes accessed | tf_op | source)
XLA Modules:
  0.0 193.5 jit_solution(12469178509080288920)
XLA Ops:
  0.0 1.3 broadcast_in_dim.8.ga_ref
  1.3 1.3 broadcast_in_dim.9.gm_ref
  2.6 0.8 multiply_sine_fusion
  3.5 187.6 %layer.1 = bf16[256,2560]{1,0:T(8,128)(2,1)} custom-call(bf16[256,2560]{1,0:T(8,128)(2,1)} %x_ref.1, f32[1,2560]{1,0:T(1,128)} %broadcast_in_dim.8.ga_ref, f32[1,2560]{1,0:T(1,128)} %broadcast_in_dim.9.gm_ref, f32[40,256]{1,0:T(8,128)} %get-tuple-element.6.cos_ref, f32[40,256]{1,0:T(8,128)} %get-tuple-element.5.sin_ref, bf16[2560,7680]{1,0:T(8,128)(2,1)} %wqkv_ref.1, ...), custom_call_target="tpu_custom_call" | custom-call | tf_op jit(solution)/shard_map/layer/pallas_call | solution.py:367
  191.1 2.5 %copy.10 = bf16[256,2560]{1,0:T(8,128)(2,1)} copy(bf16[256,2560]{1,0:T(8,128)(2,1)} %layer.1) | data formatting | bytes 2621440
  (2 shorter events, 0.0 us)

commit v3 on v2

--- a/solution.py
+++ b/solution.py
@@ -27,9 +27,9 @@
 
 
 def layer_kernel(n, hpd, hd, group, chunk, slots,
-                 x_ref, ga_ref, gm_ref, cos_ref, sin_ref, wqkv_ref, wout_ref, wg_ref, wu_ref, wd_ref, z_ref,
-                 wout, xn, kvs, kvr, qs, qr, kbuf, osend, orecv, yn, ybuf, acc, zrecv, wg, wu, wd,
-                 stage_sem, wout_sem, w_sem, kv_ss, kv_rs, q_ss, q_rs, o_ss, o_rs, y_ss, y_rs, z_ss, z_rs):
+                 xin_ref, ga_ref, gm_ref, cos_ref, sin_ref, wqkv_ref, wout_ref, wg_ref, wu_ref, wd_ref, z_ref,
+                 x_ref, wout, xn, kvs, kvr, qs, qr, kbuf, osend, orecv, yn, hidden, zown, zsend, zrecv, wbuf,
+                 x_sem, stage_sem, wout_sem, w_sem, kv_ss, kv_rs, q_ss, q_rs, o_ss, o_rs, y_ss, y_rs, z_ss, z_rs):
     rows, width = x_ref.shape
     half_rows = rows // HALVES
     inner = n * hpd * hd
@@ -37,7 +37,9 @@
     ngroups = n // group
     stages = width // gcols
     ff_half = wg_ref.shape[1] // 2
-    nchunks = ff_half // chunk
+    nup = ff_half // chunk
+    ndown = width // chunk
+    nsteps = nup + ndown
     me = lax.axis_index('seq')
     core = lax.rem(me, 2)
     partner = me + 1 - 2 * core
@@ -61,13 +63,32 @@
         def _():
             tile_copy(s, 0, s - 2 * ngroups).start()
 
-    def chunk_copies(s):
+    def up_copies(c, slot):
+        ff = pl.multiple_of(core * ff_half + c * chunk, 128)
+        return (pltpu.make_async_copy(wg_ref.at[:, pl.ds(ff, chunk)], wbuf.at[slot, 0:width], w_sem.at[slot, 0]),
+                pltpu.make_async_copy(wu_ref.at[:, pl.ds(ff, chunk)], wbuf.at[slot, width:2 * width], w_sem.at[slot, 1]))
+
+    def down_copies(c, slot):
+        col = pl.multiple_of(c * chunk, 128)
+        return tuple(pltpu.make_async_copy(wd_ref.at[pl.ds(core * ff_half + p * width, width), pl.ds(col, chunk)],
+                                           wbuf.at[slot, p * width:(p + 1) * width], w_sem.at[slot, p]) for p in range(2))
+
+    def start_step(s):
+        c = lax.rem(s, nsteps)
         slot = lax.rem(s, slots)
-        ff = pl.multiple_of(core * ff_half + lax.rem(s, nchunks) * chunk, 128)
-        return (pltpu.make_async_copy(wg_ref.at[:, pl.ds(ff, chunk)], wg.at[slot], w_sem.at[0, slot]),
-                pltpu.make_async_copy(wu_ref.at[:, pl.ds(ff, chunk)], wu.at[slot], w_sem.at[1, slot]),
-                pltpu.make_async_copy(wd_ref.at[pl.ds(ff, chunk), :], wd.at[slot], w_sem.at[2, slot]))
-
+
+        @pl.when(jnp.logical_and(c < nup, s < HALVES * nsteps))
+        def _():
+            for copy in up_copies(c, slot):
+                copy.start()
+
+        @pl.when(jnp.logical_and(c >= nup, s < HALVES * nsteps))
+        def _():
+            for copy in down_copies(c - nup, slot):
+                copy.start()
+
+    x_copy = pltpu.make_async_copy(xin_ref, x_ref, x_sem)
+    x_copy.start()
     for s in range(stages):
         start_tile(s)
 
@@ -78,8 +99,11 @@
         return c
 
     lax.fori_loop(1, n, greet, 0)
-    xn[...] = rms_norm(x_ref[...], ga_ref[...])
-    pl.semaphore_wait(barrier, n - 1)
+    def gain(ref):
+        return jnp.concatenate([ref[r:r + 1, :] for r in range(ref.shape[0])], axis=1)
+
+    x_copy.wait()
+    xn[...] = rms_norm(x_ref[...], gain(ga_ref))
 
     def remote(src, dst, ssem, rsem, dest):
         return pltpu.make_async_remote_copy(src_ref=src, dst_ref=dst, send_sem=ssem, recv_sem=rsem,
@@ -146,6 +170,10 @@
                 if t == 0:
                     u = rope(u)
                 kvs[grp_of(g) * group + k // hpd, k % hpd, t * hd:(t + 1) * hd, :] = u.astype(jnp.bfloat16)
+        @pl.when(g == 0)
+        def _():
+            pl.semaphore_wait(barrier, n - 1)
+
         send_group(g, lambda dest: kv_send(dest, 0))
         return c
 
@@ -180,8 +208,7 @@
     wout_copy = pltpu.make_async_copy(wout_ref, wout, wout_sem)
     wout_copy.start()
     for s in range(slots):
-        for copy in chunk_copies(s):
-            copy.start()
+        start_step(s)
 
     per = 4
     kv_per = 2
@@ -216,21 +243,22 @@
         def one_tile(i, c):
             q_t = jnp.concatenate([qr[per * i + r, h, f] for r in range(per)], axis=1)
 
-            def scores(j, q):
-                k_blk = kbuf[pl.ds(pl.multiple_of(j * kv_tile, kv_tile), kv_tile), :]
+            def scores(j, q, blocks=kv_per):
+                size = blocks * rows
+                k_blk = kbuf[pl.ds(pl.multiple_of(j * size, size), size), :]
                 return jnp.dot(k_blk, q, preferred_element_type=jnp.float32)
 
-            def values(j):
-                return jnp.concatenate([kvr[kv_per * j + r, h, hd:2 * hd, :] for r in range(kv_per)], axis=1)
-
-            def update(j, s, carry):
+            def values(j, blocks):
+                return jnp.concatenate([kvr[blocks * j + r, h, hd:2 * hd, :] for r in range(blocks)], axis=1)
+
+            def update(j, s, carry, blocks=kv_per):
                 m_new = jnp.max(s, axis=0, keepdims=True)
                 if carry is not None:
                     m, l, o = carry
                     m_new = jnp.maximum(m, m_new)
                 p = jnp.exp2((s - m_new) * scale2)
                 l_new = jnp.sum(p, axis=0, keepdims=True)
-                o_new = jnp.dot(values(j), p.astype(jnp.bfloat16), preferred_element_type=jnp.float32)
+                o_new = jnp.dot(values(j, blocks), p.astype(jnp.bfloat16), preferred_element_type=jnp.float32)
                 if carry is not None:
                     alpha = jnp.exp2((m - m_new) * scale2)
                     l_new = alpha * l + l_new
@@ -250,7 +278,7 @@
             cut = q_tile // diag
             late = update(diag * i + 1, masked(diag * i + 1, kv_tile, cut), tuple(v[:, cut:] for v in carry))
             carry = tuple(jnp.concatenate([v[:, :cut], w], axis=1) for v, w in zip(carry, late))
-            m, l, o = lax.fori_loop(0, diag * i, lambda j, cr: update(j, scores(j, q_t), cr), carry)
+            m, l, o = lax.fori_loop(0, i, lambda j, cr: update(j, scores(j, q_t, per), cr, per), carry)
             out = (o / l).astype(jnp.bfloat16)
             for r in range(per):
                 dest = per * i + r
@@ -283,10 +311,10 @@
     def y_send(f):
         return remote(yn.at[f, 0], yn.at[f, 1], y_ss.at[f], y_rs.at[f], partner)
 
-    def z_send(f):
-        return remote(acc.at[f, 1], zrecv.at[f], z_ss.at[f], z_rs.at[f], partner)
-
-    for f in range(HALVES):
+    def z_send(f, c):
+        return remote(zsend.at[c], zrecv.at[f, c], z_ss.at[f, c], z_rs.at[f, c], partner)
+
+    def out_projection(f):
         r0 = f * half_rows
 
         def arrive_o(k, c):
@@ -298,40 +326,58 @@
         o_rows = orecv[f].reshape(inner, half_rows).T
         mixed = jnp.dot(o_rows, wout[...], preferred_element_type=jnp.float32)
         y = (x_ref[r0:r0 + half_rows, :].astype(jnp.float32) + mixed).astype(jnp.bfloat16)
-        ybuf[r0:r0 + half_rows, :] = y
-        yn[f, 0] = rms_norm(y, gm_ref[...])
+        x_ref[r0:r0 + half_rows, :] = y
+        yn[f, 0] = rms_norm(y, gain(gm_ref))
         y_send(f).start()
-        acc[f] = jnp.zeros_like(acc[f])
-        y_send(f).wait()
-
-        def one_chunk(c, carry):
-            s = f * nchunks + c
+
+    def gate_up(f):
+        def one(c, carry):
+            s = f * nsteps + c
             slot = lax.rem(s, slots)
-            cg, cu, cd = chunk_copies(s)
+            for copy in up_copies(c, slot):
+                copy.wait()
             y_all = yn[f].reshape(2 * half_rows, width)
-            cg.wait()
-            gate = jnp.dot(y_all, wg[slot], preferred_element_type=jnp.float32)
-            cu.wait()
-            up = jnp.dot(y_all, wu[slot], preferred_element_type=jnp.float32)
-            hidden = (gate / (1.0 + jnp.exp(-gate)) * up).astype(jnp.bfloat16)
-            cd.wait()
-            part = jnp.dot(hidden, wd[slot], preferred_element_type=jnp.float32)
-            acc[f] += part.reshape(2, half_rows, width)
-
-            @pl.when(s + slots < HALVES * nchunks)
-            def _():
-                for copy in chunk_copies(s + slots):
-                    copy.start()
+            gate = jnp.dot(y_all, wbuf[slot, 0:width], preferred_element_type=jnp.float32)
+            up = jnp.dot(y_all, wbuf[slot, width:2 * width], preferred_element_type=jnp.float32)
+            hidden[:, pl.ds(pl.multiple_of(c * chunk, 128), chunk)] = (gate / (1.0 + jnp.exp(-gate)) * up).astype(jnp.bfloat16)
+            start_step(s + slots)
             return carry
 
-        lax.fori_loop(0, nchunks, one_chunk, 0)
-        z_send(f).start()
-
-    for f in range(HALVES):
+        lax.fori_loop(0, nup, one, 0)
+
+    def down(f):
+        def one(c, carry):
+            s = f * nsteps + nup + c
+            slot = lax.rem(s, slots)
+            for copy in down_copies(c, slot):
+                copy.wait()
+            part = jnp.dot(hidden[...], wbuf[slot], preferred_element_type=jnp.float32)
+            zsend[c] = part[half_rows:]
+            z_send(f, c).start()
+            zown[c] = part[:half_rows]
+            start_step(s + slots)
+            return carry
+
+        lax.fori_loop(0, ndown, one, 0)
+
+    def finish(f):
         r0 = f * half_rows
-        z_send(f).wait()
-        total = acc[f, 0] + zrecv[f]
-        z_ref[r0:r0 + half_rows, :] = (ybuf[r0:r0 + half_rows, :].astype(jnp.float32) + total).astype(jnp.bfloat16)
+        for c in range(ndown):
+            z_send(f, c).wait()
+            total = zown[c] + zrecv[f, c]
+            cols = slice(c * chunk, (c + 1) * chunk)
+            z_ref[r0:r0 + half_rows, cols] = (x_ref[r0:r0 + half_rows, cols].astype(jnp.float32) + total).astype(jnp.bfloat16)
+
+    out_projection(0)
+    y_send(0).wait()
+    gate_up(0)
+    out_projection(1)
+    down(0)
+    y_send(1).wait()
+    gate_up(1)
+    finish(0)
+    down(1)
+    finish(1)
 
     def drain(k, c):
         other = lax.rem(me + k, n)
@@ -358,7 +404,7 @@
         group = 1
         while (group * hpd * hd) % 128:
             group *= 2
-        chunk, slots = 512, 2
+        chunk, slots = 512, 4
         half = rows // HALVES
         bf16, f32 = jnp.bfloat16, jnp.float32
         vmem = pl.BlockSpec(memory_space=pltpu.VMEM)
@@ -367,9 +413,10 @@
         return pl.pallas_call(
             functools.partial(layer_kernel, n, hpd, hd, group, chunk, slots),
             out_shape=jax.ShapeDtypeStruct(x_blk.shape, bf16),
-            in_specs=[vmem] * 5 + [hbm] * 5,
+            in_specs=[hbm] + [vmem] * 4 + [hbm] * 5,
             out_specs=vmem,
             scratch_shapes=[
+                pltpu.VMEM((rows, width), bf16),
                 pltpu.VMEM((n_heads * hd, width), bf16),
                 pltpu.VMEM((rows, width), bf16),
                 pltpu.VMEM((n, hpd, 2 * hd, rows), bf16),
@@ -380,19 +427,18 @@
                 pltpu.VMEM((HALVES, n, hpd, hd, half), bf16),
                 pltpu.VMEM((HALVES, n, hpd, hd, half), bf16),
                 pltpu.VMEM((HALVES, 2, half, width), bf16),
-                pltpu.VMEM((rows, width), bf16),
-                pltpu.VMEM((HALVES, 2, half, width), f32),
-                pltpu.VMEM((HALVES, half, width), f32),
-                pltpu.VMEM((slots, width, chunk), bf16),
-                pltpu.VMEM((slots, width, chunk), bf16),
-                pltpu.VMEM((slots, chunk, width), bf16),
-                dma((4,)), dma, dma((3, slots)),
+                pltpu.VMEM((rows, w_down.shape[0] // 2), bf16),
+                pltpu.VMEM((width // chunk, half, chunk), f32),
+                pltpu.VMEM((width // chunk, half, chunk), f32),
+                pltpu.VMEM((HALVES, width // chunk, half, chunk), f32),
+                pltpu.VMEM((slots, 2 * width, chunk), bf16),
+                dma, dma((4,)), dma, dma((slots, 2)),
                 dma((n, hpd)), dma((n, hpd)), dma((n, 3)), dma((n, 3)), dma((HALVES, n)), dma((HALVES, n)),
-                dma((HALVES,)), dma((HALVES,)), dma((HALVES,)), dma((HALVES,)),
+                dma((HALVES,)), dma((HALVES,)), dma((HALVES, width // chunk)), dma((HALVES, width // chunk)),
             ],
             compiler_params=pltpu.CompilerParams(collective_id=0, has_side_effects=True, vmem_limit_bytes=67043328),
             name='layer',
-        )(x_blk, g_attn[None, :], g_mlp[None, :], cos_t, sin_t, w_qkv, w_out.reshape(n_heads * hd, width), w_gate, w_up, w_down)
+        )(x_blk, g_attn.reshape(-1, 128), g_mlp.reshape(-1, 128), cos_t, sin_t, w_qkv, w_out.reshape(n_heads * hd, width), w_gate, w_up, w_down)
 
     row_spec = P(('data', 'seq'), None)
     return jax.shard_map(local_layer, mesh=mesh, in_specs=(row_spec, P(), P(), P(), P(), P(), P(), P()), out_specs=row_spec, check_vma=False)

time: 194 us -> 181 us (0.933)
  Pallas kernels: 188 us -> 177 us
  local copies, waits for them, and re-layouts: 5.08 us -> 2.46 us
    pallas_call x1, Pallas kernels: 188 us -> 177 us  [local_layer(): pl.pallas_call(functools.partial(layer_kernel, n, hpd, hd, group, chunk,...]
    broadcast_in_dim x2 -> x0, local copies, waits for them, and re-layouts: 2.62 us -> none  [the longest x1 1.31 us: local_layer(): g_attn[None, :]]
where the time goes in v3:
time: 181 us
  Pallas kernels  177 us (98%)
  local copies, waits for them, and re-layouts  2.46 us (1%)
    pallas_call x1, Pallas kernels, local_layer(): pl.pallas_call(functools.partial(layer_kernel, n, hpd, hd, group, chunk,...  177 us

profile of v3, /device:TPU:21, one launch (start us, length us, event | category | flops | bytes accessed | tf_op | source)
XLA Modules:
  0.0 180.8 jit_solution(12976029226781093004)
XLA Ops:
  0.0 0.9 multiply_sine_fusion
  0.9 177.5 %layer.1 = bf16[256,2560]{1,0:T(8,128)(2,1)} custom-call(bf16[256,2560]{1,0:T(8,128)(2,1)} %xin_ref.1, f32[20,128]{1,0:T(8,128)} %bitcast.4, f32[20,128]{1,0:T(8,128)} %bitcast.5, f32[40,256]{1,0:T(8,128)} %get-tuple-element.6.cos_ref, f32[40,256]{1,0:T(8,128)} %get-tuple-element.5.sin_ref, bf16[2560,7680]{1,0:T(8,128)(2,1)} %wqkv_ref.1, ...), custom_call_target="tpu_custom_call" | custom-call | tf_op jit(solution)/shard_map/layer/pallas_call | solution.py:413
  178.4 2.5 %copy.10 = bf16[256,2560]{1,0:T(8,128)(2,1)} copy(bf16[256,2560]{1,0:T(8,128)(2,1)} %layer.1) | data formatting | bytes 2621440
  (2 shorter events, 0.0 us)

commit v4 on v3

--- a/solution.py
+++ b/solution.py
@@ -27,9 +27,9 @@
 
 
 def layer_kernel(n, hpd, hd, group, chunk, slots,
-                 xin_ref, ga_ref, gm_ref, cos_ref, sin_ref, wqkv_ref, wout_ref, wg_ref, wu_ref, wd_ref, z_ref,
-                 x_ref, wout, xn, kvs, kvr, qs, qr, kbuf, osend, orecv, yn, hidden, zown, zsend, zrecv, wbuf,
-                 x_sem, stage_sem, wout_sem, w_sem, kv_ss, kv_rs, q_ss, q_rs, o_ss, o_rs, y_ss, y_rs, z_ss, z_rs):
+                 xin_ref, gain_refs, gainm_refs, cosin_ref, sinin_ref, wqkv_ref, wout_ref, wg_ref, wu_ref, wd_ref, z_ref,
+                 x_ref, ga_ref, gm_ref, cos_ref, sin_ref, wout, kvs, kvr, qs, qr, kbuf, osend, orecv, yn, hidden, zown, zsend, zrecv, wbuf,
+                 in_sem, stage_sem, wout_sem, w_sem, kv_ss, kv_rs, q_ss, q_rs, o_ss, o_rs, y_ss, y_rs, z_ss, z_rs):
     rows, width = x_ref.shape
     half_rows = rows // HALVES
     inner = n * hpd * hd
@@ -45,8 +45,13 @@
     partner = me + 1 - 2 * core
     mygrp = me // group
 
+    order = sorted(range(ngroups), key=lambda d: -min(d, ngroups - d))
+
     def grp_of(g):
-        return lax.rem(mygrp + ngroups // 2 + g, ngroups)
+        off = 0
+        for i, d in enumerate(order):
+            off = jnp.where(g == i, d, off)
+        return lax.rem(mygrp + off, ngroups)
 
     def tile_copy(s, t, g):
         col = pl.multiple_of(t * inner + grp_of(g) * gcols, 128)
@@ -73,24 +78,25 @@
         return tuple(pltpu.make_async_copy(wd_ref.at[pl.ds(core * ff_half + p * width, width), pl.ds(col, chunk)],
                                            wbuf.at[slot, p * width:(p + 1) * width], w_sem.at[slot, p]) for p in range(2))
 
-    def start_step(s):
-        c = lax.rem(s, nsteps)
-        slot = lax.rem(s, slots)
-
-        @pl.when(jnp.logical_and(c < nup, s < HALVES * nsteps))
-        def _():
-            for copy in up_copies(c, slot):
-                copy.start()
-
-        @pl.when(jnp.logical_and(c >= nup, s < HALVES * nsteps))
-        def _():
-            for copy in down_copies(c - nup, slot):
-                copy.start()
-
-    x_copy = pltpu.make_async_copy(xin_ref, x_ref, x_sem)
-    x_copy.start()
+    def start_up(c):
+        for copy in up_copies(c, lax.rem(c, slots)):
+            copy.start()
+
+    def down_slot(c):
+        return slots - 1 - lax.rem(c, slots)
+
+    def start_down(c):
+        for copy in down_copies(c, down_slot(c)):
+            copy.start()
+
+    inputs = [pltpu.make_async_copy(src, dst, in_sem.at[i]) for i, (src, dst) in enumerate(
+        [(xin_ref, x_ref), (gain_refs, ga_ref), (cosin_ref, cos_ref), (sinin_ref, sin_ref), (gainm_refs, gm_ref)])]
+    inputs[0].start()
+    inputs[1].start()
     for s in range(stages):
         start_tile(s)
+    for copy in inputs[2:]:
+        copy.start()
 
     barrier = pltpu.get_barrier_semaphore()
 
@@ -102,21 +108,27 @@
     def gain(ref):
         return jnp.concatenate([ref[r:r + 1, :] for r in range(ref.shape[0])], axis=1)
 
-    x_copy.wait()
-    xn[...] = rms_norm(x_ref[...], gain(ga_ref))
+    inputs[0].wait()
+    inputs[1].wait()
+    yn[1] = rms_norm(x_ref[...], gain(ga_ref)).reshape(2, half_rows, width)
+    for copy in inputs[2:]:
+        copy.wait()
 
     def remote(src, dst, ssem, rsem, dest):
         return pltpu.make_async_remote_copy(src_ref=src, dst_ref=dst, send_sem=ssem, recv_sem=rsem,
                                             device_id={'seq': dest}, device_id_type=MESH)
 
-    def kv_send(dest, h):
-        return remote(kvs.at[dest, h], kvr.at[me, h], kv_ss.at[dest, h], kv_rs.at[me, h], dest)
-
-    def kv_recv(src, h):
-        return remote(kvs.at[src, h], kvr.at[src, h], kv_ss.at[src, h], kv_rs.at[src, h], src)
-
-    def kv_local(h):
-        return pltpu.make_async_copy(kvs.at[me, h], kvr.at[me, h], kv_rs.at[me, h])
+    def kv_part(ref, u):
+        return ref.at[1] if u == 2 else ref.at[0, u * hd:(u + 1) * hd]
+
+    def kv_send(dest, u):
+        return remote(kv_part(kvs.at[dest], u), kv_part(kvr.at[me], u), kv_ss.at[dest, u], kv_rs.at[me, u], dest)
+
+    def kv_recv(src, u):
+        return remote(kv_part(kvs.at[src], u), kv_part(kvr.at[src], u), kv_ss.at[src, u], kv_rs.at[src, u], src)
+
+    def kv_local(u):
+        return pltpu.make_async_copy(kv_part(kvs.at[me], u), kv_part(kvr.at[me], u), kv_rs.at[me, u])
 
     def q_send(dest, u):
         src, dst = (qs.at[dest, 0], qr.at[me, 0]) if u == 0 else (qs.at[dest, 1, u - 1], qr.at[me, 1, u - 1])
@@ -141,7 +153,7 @@
 
     def project(s):
         start = pl.multiple_of(lax.rem(s, stages) * gcols, 128)
-        out = jnp.dot(xn[...], wout[:, pl.ds(start, gcols)], preferred_element_type=jnp.float32)
+        out = jnp.dot(yn[1].reshape(rows, width), wout[:, pl.ds(start, gcols)], preferred_element_type=jnp.float32)
         start_tile(s + stages)
         return out.T
 
@@ -170,16 +182,17 @@
                 if t == 0:
                     u = rope(u)
                 kvs[grp_of(g) * group + k // hpd, k % hpd, t * hd:(t + 1) * hd, :] = u.astype(jnp.bfloat16)
-        @pl.when(g == 0)
-        def _():
-            pl.semaphore_wait(barrier, n - 1)
-
-        send_group(g, lambda dest: kv_send(dest, 0))
+            if t == 0:
+                @pl.when(g == 0)
+                def _():
+                    pl.semaphore_wait(barrier, n - 1)
+
+            send_group(g, lambda dest: kv_send(dest, t))
         return c
 
     lax.fori_loop(0, ngroups, project_kv, 0)
-    kv_local(0).start()
-    kv_local(1).start()
+    for u in range(3):
+        kv_local(u).start()
 
     def project_q(g, c):
         s = 2 * ngroups + g
@@ -203,12 +216,12 @@
 
         lax.fori_loop(1, n, one, 0)
 
-    to_others(lambda dest: kv_send(dest, 1))
+    to_others(lambda dest: kv_send(dest, 2))
 
     wout_copy = pltpu.make_async_copy(wout_ref, wout, wout_sem)
     wout_copy.start()
-    for s in range(slots):
-        start_step(s)
+    for c in range(slots):
+        start_up(c)
 
     per = 4
     kv_per = 2
@@ -218,13 +231,14 @@
 
     def arrive_kv(h):
         def one(src, c):
-            @pl.when(src != me)
-            def _():
-                kv_recv(src, h).wait_recv()
-
-            @pl.when(src == me)
-            def _():
-                kv_local(h).wait()
+            for u in ((0, 1) if h == 0 else (2,)):
+                @pl.when(src != me)
+                def _():
+                    kv_recv(src, u).wait_recv()
+
+                @pl.when(src == me)
+                def _():
+                    kv_local(u).wait()
 
             kbuf[pl.ds(pl.multiple_of(src * rows, rows), rows), :] = kvr[src, h, 0:hd, :].T
             return c
@@ -311,8 +325,8 @@
     def y_send(f):
         return remote(yn.at[f, 0], yn.at[f, 1], y_ss.at[f], y_rs.at[f], partner)
 
-    def z_send(f, c):
-        return remote(zsend.at[c], zrecv.at[f, c], z_ss.at[f, c], z_rs.at[f, c], partner)
+    def z_send(c):
+        return remote(zsend.at[c], zrecv.at[c], z_ss.at[c], z_rs.at[c], partner)
 
     def out_projection(f):
         r0 = f * half_rows
@@ -330,60 +344,81 @@
         yn[f, 0] = rms_norm(y, gain(gm_ref))
         y_send(f).start()
 
-    def gate_up(f):
-        def one(c, carry):
-            s = f * nsteps + c
-            slot = lax.rem(s, slots)
-            for copy in up_copies(c, slot):
-                copy.wait()
+    def gate_up(f, first, last):
+        def one(t, carry):
+            c = t if f == 0 else nup - 1 - t
+            slot = lax.rem(c, slots)
+            if f == 0:
+                for copy in up_copies(c, slot):
+                    copy.wait()
+            else:
+                @pl.when(t >= slots)
+                def _():
+                    for copy in up_copies(c, slot):
+                        copy.wait()
             y_all = yn[f].reshape(2 * half_rows, width)
             gate = jnp.dot(y_all, wbuf[slot, 0:width], preferred_element_type=jnp.float32)
             up = jnp.dot(y_all, wbuf[slot, width:2 * width], preferred_element_type=jnp.float32)
-            hidden[:, pl.ds(pl.multiple_of(c * chunk, 128), chunk)] = (gate / (1.0 + jnp.exp(-gate)) * up).astype(jnp.bfloat16)
-            start_step(s + slots)
+            cols = pl.ds(pl.multiple_of(c * chunk, 128), chunk)
+            hidden[f, :, cols] = (gate / (1.0 + jnp.exp(-gate)) * up).astype(jnp.bfloat16)
+            if f == 0:
+                @pl.when(c + slots < nup)
+                def _():
+                    start_up(c + slots)
+            else:
+                @pl.when(c >= slots)
+                def _():
+                    start_up(c - slots)
+
+                @pl.when(c < slots)
+                def _():
+                    start_down(slots - 1 - c)
             return carry
 
-        lax.fori_loop(0, nup, one, 0)
-
-    def down(f):
+        lax.fori_loop(first, last, one, 0)
+
+    def down(first, last):
         def one(c, carry):
-            s = f * nsteps + nup + c
-            slot = lax.rem(s, slots)
+            slot = down_slot(c)
             for copy in down_copies(c, slot):
                 copy.wait()
-            part = jnp.dot(hidden[...], wbuf[slot], preferred_element_type=jnp.float32)
-            zsend[c] = part[half_rows:]
-            z_send(f, c).start()
-            zown[c] = part[:half_rows]
-            start_step(s + slots)
+            part = jnp.dot(hidden[...].reshape(HALVES * rows, ff_half), wbuf[slot], preferred_element_type=jnp.float32)
+            part = part.reshape(HALVES, 2, half_rows, chunk)
+            zsend[c] = part[:, 1]
+            z_send(c).start()
+            zown[c] = part[:, 0]
+
+            @pl.when(c + slots < ndown)
+            def _():
+                start_down(c + slots)
             return carry
 
-        lax.fori_loop(0, ndown, one, 0)
-
-    def finish(f):
-        r0 = f * half_rows
-        for c in range(ndown):
-            z_send(f, c).wait()
-            total = zown[c] + zrecv[f, c]
-            cols = slice(c * chunk, (c + 1) * chunk)
-            z_ref[r0:r0 + half_rows, cols] = (x_ref[r0:r0 + half_rows, cols].astype(jnp.float32) + total).astype(jnp.bfloat16)
+        lax.fori_loop(first, last, one, 0)
+
+    def finish(c):
+        z_send(c).wait()
+        cols = slice(c * chunk, (c + 1) * chunk)
+        total = (zown[c] + zrecv[c]).reshape(rows, chunk)
+        z_ref[:, cols] = (x_ref[:, cols].astype(jnp.float32) + total).astype(jnp.bfloat16)
 
     out_projection(0)
     y_send(0).wait()
-    gate_up(0)
+    gate_up(0, 0, nup - 2)
     out_projection(1)
-    down(0)
+    gate_up(0, nup - 2, nup)
     y_send(1).wait()
-    gate_up(1)
-    finish(0)
-    down(1)
-    finish(1)
+    gate_up(1, 0, nup)
+    down(0, ndown - 1)
+    for c in range(ndown - 2):
+        finish(c)
+    down(ndown - 1, ndown)
+    for c in range(ndown - 2, ndown):
+        finish(c)
 
     def drain(k, c):
         other = lax.rem(me + k, n)
-        for h in range(hpd):
-            kv_send(other, h).wait_send()
         for u in range(3):
+            kv_send(other, u).wait_send()
             q_send(other, u).wait_send()
         for f in range(HALVES):
             o_send(other, f).wait_send()
@@ -404,7 +439,7 @@
         group = 1
         while (group * hpd * hd) % 128:
             group *= 2
-        chunk, slots = 512, 4
+        chunk, slots = 512, 3
         half = rows // HALVES
         bf16, f32 = jnp.bfloat16, jnp.float32
         vmem = pl.BlockSpec(memory_space=pltpu.VMEM)
@@ -412,13 +447,16 @@
         dma = pltpu.SemaphoreType.DMA
         return pl.pallas_call(
             functools.partial(layer_kernel, n, hpd, hd, group, chunk, slots),
-            out_shape=jax.ShapeDtypeStruct(x_blk.shape, bf16),
-            in_specs=[hbm] + [vmem] * 4 + [hbm] * 5,
+            out_shape=pltpu.VMEM(x_blk.shape, bf16),
+            in_specs=[hbm] * 10,
             out_specs=vmem,
             scratch_shapes=[
                 pltpu.VMEM((rows, width), bf16),
+                pltpu.VMEM((width // 128, 128), f32),
+                pltpu.VMEM((width // 128, 128), f32),
+                pltpu.VMEM((hd // 2, rows), f32),
+                pltpu.VMEM((hd // 2, rows), f32),
                 pltpu.VMEM((n_heads * hd, width), bf16),
-                pltpu.VMEM((rows, width), bf16),
                 pltpu.VMEM((n, hpd, 2 * hd, rows), bf16),
                 pltpu.VMEM((n, hpd, 2 * hd, rows), bf16),
                 pltpu.VMEM((n, hpd, HALVES, hd, half), bf16),
@@ -427,16 +465,16 @@
                 pltpu.VMEM((HALVES, n, hpd, hd, half), bf16),
                 pltpu.VMEM((HALVES, n, hpd, hd, half), bf16),
                 pltpu.VMEM((HALVES, 2, half, width), bf16),
-                pltpu.VMEM((rows, w_down.shape[0] // 2), bf16),
-                pltpu.VMEM((width // chunk, half, chunk), f32),
-                pltpu.VMEM((width // chunk, half, chunk), f32),
-                pltpu.VMEM((HALVES, width // chunk, half, chunk), f32),
+                pltpu.VMEM((HALVES, rows, w_down.shape[0] // 2), bf16),
+                pltpu.VMEM((width // chunk, HALVES, half, chunk), f32),
+                pltpu.VMEM((width // chunk, HALVES, half, chunk), f32),
+                pltpu.VMEM((width // chunk, HALVES, half, chunk), f32),
                 pltpu.VMEM((slots, 2 * width, chunk), bf16),
-                dma, dma((4,)), dma, dma((slots, 2)),
-                dma((n, hpd)), dma((n, hpd)), dma((n, 3)), dma((n, 3)), dma((HALVES, n)), dma((HALVES, n)),
-                dma((HALVES,)), dma((HALVES,)), dma((HALVES, width // chunk)), dma((HALVES, width // chunk)),
+                dma((5,)), dma((4,)), dma, dma((slots, 2)),
+                dma((n, 3)), dma((n, 3)), dma((n, 3)), dma((n, 3)), dma((HALVES, n)), dma((HALVES, n)),
+                dma((HALVES,)), dma((HALVES,)), dma((width // chunk,)), dma((width // chunk,)),
             ],
-            compiler_params=pltpu.CompilerParams(collective_id=0, has_side_effects=True, vmem_limit_bytes=67043328),
+            compiler_params=pltpu.CompilerParams(collective_id=0, has_side_effects=True, vmem_limit_bytes=64 * 1000 * 1024),
             name='layer',
         )(x_blk, g_attn.reshape(-1, 128), g_mlp.reshape(-1, 128), cos_t, sin_t, w_qkv, w_out.reshape(n_heads * hd, width), w_gate, w_up, w_down)
 

time: 181 us -> 175 us (0.967); the launches traced: 181 us -> 173 us
  Pallas kernels: 177 us -> 171 us
    pallas_call x1, Pallas kernels: 177 us -> 171 us  [local_layer(): pl.pallas_call(functools.partial(layer_kernel, n, hpd, hd, group, chunk,...]
where the time goes in v4:
time: 175 us; the launch traced here: 173 us
  Pallas kernels  171 us (98%)
    pallas_call x1, Pallas kernels, local_layer(): pl.pallas_call(functools.partial(layer_kernel, n, hpd, hd, group, chunk,...  171 us

profile of v4, /device:TPU:21, one launch (start us, length us, event | category | flops | bytes accessed | tf_op | source)
XLA Modules:
  0.0 172.8 jit_solution(14671302720622240726)
XLA Ops:
  0.0 0.9 multiply_sine_fusion
  0.9 170.9 %layer.1 = bf16[256,2560]{1,0:T(8,128)(2,1)S(1)} custom-call(bf16[256,2560]{1,0:T(8,128)(2,1)} %xin_ref.1, f32[20,128]{1,0:T(8,128)} %bitcast.4, f32[20,128]{1,0:T(8,128)} %bitcast.5, f32[40,256]{1,0:T(8,128)} %get-tuple-element.6.cosin_ref, f32[40,256]{1,0:T(8,128)} %get-tuple-element.5.sinin_ref, bf16[2560,7680]{1,0:T(8,128)(2,1)} %wqkv_ref.1, ...), custom_call_target="tpu_custom_call" | custom-call | tf_op jit(solution)/shard_map/layer/pallas_call | solution.py:448
  171.8 1.1 copy.10
  (2 shorter events, 0.0 us)

commit v5 on v4

--- a/solution.py
+++ b/solution.py
@@ -28,7 +28,7 @@
 
 def layer_kernel(n, hpd, hd, group, chunk, slots,
                  xin_ref, gain_refs, gainm_refs, cosin_ref, sinin_ref, wqkv_ref, wout_ref, wg_ref, wu_ref, wd_ref, z_ref,
-                 x_ref, ga_ref, gm_ref, cos_ref, sin_ref, wout, kvs, kvr, qs, qr, kbuf, osend, orecv, yn, hidden, zown, zsend, zrecv, wbuf,
+                 x_ref, ga_ref, gm_ref, cos_ref, sin_ref, wout, kvs, kvr, qs, qr, kbuf, sbuf, osend, orecv, yn, hidden, zown, zsend, zrecv, wbuf,
                  in_sem, stage_sem, wout_sem, w_sem, kv_ss, kv_rs, q_ss, q_rs, o_ss, o_rs, y_ss, y_rs, z_ss, z_rs):
     rows, width = x_ref.shape
     half_rows = rows // HALVES
@@ -83,7 +83,7 @@
             copy.start()
 
     def down_slot(c):
-        return slots - 1 - lax.rem(c, slots)
+        return slots - 1 - c % slots
 
     def start_down(c):
         for copy in down_copies(c, down_slot(c)):
@@ -111,8 +111,6 @@
     inputs[0].wait()
     inputs[1].wait()
     yn[1] = rms_norm(x_ref[...], gain(ga_ref)).reshape(2, half_rows, width)
-    for copy in inputs[2:]:
-        copy.wait()
 
     def remote(src, dst, ssem, rsem, dest):
         return pltpu.make_async_remote_copy(src_ref=src, dst_ref=dst, send_sem=ssem, recv_sem=rsem,
@@ -177,6 +175,11 @@
         for t in (0, 1):
             tile_copy(2 * g + t, 1 + t, g).wait()
             out = project(2 * g + t)
+            if t == 0:
+                @pl.when(g == 0)
+                def _():
+                    inputs[2].wait()
+                    inputs[3].wait()
             for k in range(group * hpd):
                 u = out[k * hd:(k + 1) * hd]
                 if t == 0:
@@ -279,20 +282,28 @@
                     o_new = alpha * o + o_new
                 return m_new, l_new, o_new
 
-            def masked(j, off, lane0):
-                q = q_t[:, lane0:]
-                s = scores(j, q)
+            def masked(s, off, lane0):
                 lane = lane0 + lax.broadcasted_iota(jnp.int32, s.shape, 1)
                 query_pos = (lane // half_rows) * rows + f * half_rows + lane % half_rows
                 key_pos = off + lax.broadcasted_iota(jnp.int32, s.shape, 0)
                 return jnp.where(key_pos <= query_pos, s, -jnp.inf)
 
             diag = per // kv_per
-            carry = update(diag * i, masked(diag * i, 0, 0), None)
             cut = q_tile // diag
-            late = update(diag * i + 1, masked(diag * i + 1, kv_tile, cut), tuple(v[:, cut:] for v in carry))
+            first = scores(diag * i, q_t)
+            sbuf[1, :, cut:] = scores(diag * i + 1, q_t[:, cut:])
+            sbuf[0] = scores(0, q_t)
+            carry = update(diag * i, masked(first, 0, 0), None)
+            late = update(diag * i + 1, masked(sbuf[1, :, cut:], kv_tile, cut), tuple(v[:, cut:] for v in carry))
             carry = tuple(jnp.concatenate([v[:, :cut], w], axis=1) for v, w in zip(carry, late))
-            m, l, o = lax.fori_loop(0, i, lambda j, cr: update(j, scores(j, q_t, per), cr, per), carry)
+            def pair(t, carry):
+                for side in range(2):
+                    j = 2 * t + side
+                    sbuf[1 - side] = scores(j + 1, q_t)
+                    carry = update(j, sbuf[side], carry)
+                return carry
+
+            m, l, o = lax.fori_loop(0, diag * i // 2, pair, carry)
             out = (o / l).astype(jnp.bfloat16)
             for r in range(per):
                 dest = per * i + r
@@ -321,6 +332,7 @@
     arrive_q(2)
     attend(1, 1)
     wout_copy.wait()
+    inputs[4].wait()
 
     def y_send(f):
         return remote(yn.at[f, 0], yn.at[f, 1], y_ss.at[f], y_rs.at[f], partner)
@@ -401,9 +413,23 @@
         total = (zown[c] + zrecv[c]).reshape(rows, chunk)
         z_ref[:, cols] = (x_ref[:, cols].astype(jnp.float32) + total).astype(jnp.bfloat16)
 
+    def early(r):
+        for c in range(2):
+            if r == 0:
+                for copy in up_copies(c, c):
+                    copy.wait()
+            gate = jnp.dot(yn[0, r], wbuf[c, 0:width], preferred_element_type=jnp.float32)
+            up = jnp.dot(yn[0, r], wbuf[c, width:2 * width], preferred_element_type=jnp.float32)
+            silu = gate / (1.0 + jnp.exp(-gate))
+            hidden[0, r * half_rows:(r + 1) * half_rows, c * chunk:(c + 1) * chunk] = (silu * up).astype(jnp.bfloat16)
+            if r == 1:
+                start_up(c + slots)
+
     out_projection(0)
+    early(0)
     y_send(0).wait()
-    gate_up(0, 0, nup - 2)
+    early(1)
+    gate_up(0, 2, nup - 2)
     out_projection(1)
     gate_up(0, nup - 2, nup)
     y_send(1).wait()
@@ -411,7 +437,15 @@
     down(0, ndown - 1)
     for c in range(ndown - 2):
         finish(c)
-    down(ndown - 1, ndown)
+    last = ndown - 1
+    for copy in down_copies(last, down_slot(last)):
+        copy.wait()
+    for r, dst in ((1, zsend), (0, zown)):
+        rows_in = hidden[:, r * half_rows:(r + 1) * half_rows, :].reshape(HALVES * half_rows, ff_half)
+        part = jnp.dot(rows_in, wbuf[down_slot(last)], preferred_element_type=jnp.float32)
+        dst[last] = part.reshape(HALVES, half_rows, chunk)
+        if r == 1:
+            z_send(last).start()
     for c in range(ndown - 2, ndown):
         finish(c)
 
@@ -462,6 +496,7 @@
                 pltpu.VMEM((n, hpd, HALVES, hd, half), bf16),
                 pltpu.VMEM((n, hpd, HALVES, hd, half), bf16),
                 pltpu.VMEM((n * rows, hd), bf16),
+                pltpu.VMEM((2, 2 * rows, 4 * half), f32),
                 pltpu.VMEM((HALVES, n, hpd, hd, half), bf16),
                 pltpu.VMEM((HALVES, n, hpd, hd, half), bf16),
                 pltpu.VMEM((HALVES, 2, half, width), bf16),

time: 175 us -> 171 us (0.977)
  the two profiles are of different devices: /device:TPU:21 before, /device:TPU:183 now
where the time goes in v5:
time: 171 us
  Pallas kernels  169 us (99%)
    pallas_call x1, Pallas kernels, local_layer(): pl.pallas_call(functools.partial(layer_kernel, n, hpd, hd, group, chunk,...  169 us

profile of v5, /device:TPU:183, one launch (start us, length us, event | category | flops | bytes accessed | tf_op | source)
XLA Modules:
  0.0 171.3 jit_solution(8395688310932444872)
XLA Ops:
  0.0 0.9 multiply_sine_fusion
  0.9 169.3 %layer.1 = bf16[256,2560]{1,0:T(8,128)(2,1)S(1)} custom-call(bf16[256,2560]{1,0:T(8,128)(2,1)} %xin_ref.1, f32[20,128]{1,0:T(8,128)} %bitcast.4, f32[20,128]{1,0:T(8,128)} %bitcast.5, f32[40,256]{1,0:T(8,128)} %get-tuple-element.6.cosin_ref, f32[40,256]{1,0:T(8,128)} %get-tuple-element.5.sinin_ref, bf16[2560,7680]{1,0:T(8,128)(2,1)} %wqkv_ref.1, ...), custom_call_target="tpu_custom_call" | custom-call | tf_op jit(solution)/shard_map/layer/pallas_call | solution.py:482
  170.2 1.1 copy.10
  (2 shorter events, 0.0 us)

commit v6 on v5

--- a/solution.py
+++ b/solution.py
@@ -3,6 +3,7 @@
 
 import jax
 import jax.numpy as jnp
+import numpy as np
 from jax import lax
 from jax.experimental import pallas as pl
 from jax.experimental.pallas import tpu as pltpu
@@ -20,15 +21,17 @@
     return (rows_f32 * inv_rms * gain_vec).astype(jnp.bfloat16)
 
 
-def rope_tables_t(positions, head_dim):
-    inv_freq = 1.0 / (ROPE_BASE ** (jnp.arange(0, head_dim, 2, dtype=jnp.float32) / head_dim))
-    angles = inv_freq[:, None] * positions.astype(jnp.float32)[None, :]
-    return jnp.cos(angles), jnp.sin(angles)
+def rope_parts(n, rows, head_dim):
+    freq = 1.0 / (float(ROPE_BASE) ** (np.arange(0, head_dim, 2, dtype=np.float64) / head_dim))
+    local = freq[:, None] * np.arange(rows)
+    start = np.zeros((head_dim // 2, 128))
+    start[:, :n] = freq[:, None] * (np.arange(n) * rows)
+    return tuple(np.stack([np.cos(v), np.sin(v)]).astype(np.float32) for v in (local, start))
 
 
 def layer_kernel(n, hpd, hd, group, chunk, slots,
-                 xin_ref, gain_refs, gainm_refs, cosin_ref, sinin_ref, wqkv_ref, wout_ref, wg_ref, wu_ref, wd_ref, z_ref,
-                 x_ref, ga_ref, gm_ref, cos_ref, sin_ref, wout, kvs, kvr, qs, qr, kbuf, sbuf, osend, orecv, yn, hidden, zown, zsend, zrecv, wbuf,
+                 xin_ref, gain_refs, gainm_refs, angle_ref, start_ref, wqkv_ref, wout_ref, wg_ref, wu_ref, wd_ref, z_ref,
+                 x_ref, ga_ref, gm_ref, angle, angle0, cos_ref, sin_ref, wout, kvs, kvr, qs, qr, kbuf, sbuf, osend, orecv, yn, hidden, zown, zsend, zrecv, wbuf,
                  in_sem, stage_sem, wout_sem, w_sem, kv_ss, kv_rs, q_ss, q_rs, o_ss, o_rs, y_ss, y_rs, z_ss, z_rs):
     rows, width = x_ref.shape
     half_rows = rows // HALVES
@@ -90,7 +93,7 @@
             copy.start()
 
     inputs = [pltpu.make_async_copy(src, dst, in_sem.at[i]) for i, (src, dst) in enumerate(
-        [(xin_ref, x_ref), (gain_refs, ga_ref), (cosin_ref, cos_ref), (sinin_ref, sin_ref), (gainm_refs, gm_ref)])]
+        [(xin_ref, x_ref), (gain_refs, ga_ref), (angle_ref, angle), (start_ref, angle0), (gainm_refs, gm_ref)])]
     inputs[0].start()
     inputs[1].start()
     for s in range(stages):
@@ -180,6 +183,10 @@
                 def _():
                     inputs[2].wait()
                     inputs[3].wait()
+                    mine = lax.broadcasted_iota(jnp.int32, angle0.shape, 2) == me
+                    c0, s0 = jnp.sum(jnp.where(mine, angle0[...], 0.0), axis=2, keepdims=True)
+                    cos_ref[...] = angle[0] * c0 - angle[1] * s0
+                    sin_ref[...] = angle[1] * c0 + angle[0] * s0
             for k in range(group * hpd):
                 u = out[k * hd:(k + 1) * hd]
                 if t == 0:
@@ -308,17 +315,12 @@
             for r in range(per):
                 dest = per * i + r
                 osend[f, dest, h] = out[:, r * half_rows:(r + 1) * half_rows]
-                if h == hpd - 1:
-                    @pl.when(dest != me)
-                    def _():
-                        o_send(dest, f).start()
-
-                    @pl.when(dest == me)
-                    def _():
-                        o_local(f).start()
             return c
 
         lax.fori_loop(0, n // per, one_tile, 0)
+        if h == hpd - 1:
+            to_others(lambda dest: o_send(dest, f))
+            o_local(f).start()
 
     arrive_q(0)
     to_others(lambda dest: q_send(dest, 1))
@@ -468,8 +470,7 @@
         n_heads, hd, width = w_out.shape
         rows = x_blk.shape[0]
         hpd = n_heads // n
-        member = lax.axis_index('seq')
-        cos_t, sin_t = rope_tables_t(member * rows + jnp.arange(rows), hd)
+        angles, starts = (jnp.asarray(v) for v in rope_parts(n, rows, hd))
         group = 1
         while (group * hpd * hd) % 128:
             group *= 2
@@ -488,6 +489,8 @@
                 pltpu.VMEM((rows, width), bf16),
                 pltpu.VMEM((width // 128, 128), f32),
                 pltpu.VMEM((width // 128, 128), f32),
+                pltpu.VMEM((2, hd // 2, rows), f32),
+                pltpu.VMEM((2, hd // 2, 128), f32),
                 pltpu.VMEM((hd // 2, rows), f32),
                 pltpu.VMEM((hd // 2, rows), f32),
                 pltpu.VMEM((n_heads * hd, width), bf16),
@@ -511,7 +514,7 @@
             ],
             compiler_params=pltpu.CompilerParams(collective_id=0, has_side_effects=True, vmem_limit_bytes=64 * 1000 * 1024),
             name='layer',
-        )(x_blk, g_attn.reshape(-1, 128), g_mlp.reshape(-1, 128), cos_t, sin_t, w_qkv, w_out.reshape(n_heads * hd, width), w_gate, w_up, w_down)
+        )(x_blk, g_attn.reshape(-1, 128), g_mlp.reshape(-1, 128), angles, starts, w_qkv, w_out.reshape(n_heads * hd, width), w_gate, w_up, w_down)
 
     row_spec = P(('data', 'seq'), None)
     return jax.shard_map(local_layer, mesh=mesh, in_specs=(row_spec, P(), P(), P(), P(), P(), P(), P()), out_specs=row_spec, check_vma=False)

time: 171 us -> 177 us (1.035)
  the two profiles are of different devices: /device:TPU:183 before, /device:TPU:21 now
where the time goes in v6:
time: 177 us; the launch traced here: 175 us
  Pallas kernels  174 us (98%)
    pallas_call x1, Pallas kernels, local_layer(): pl.pallas_call(functools.partial(layer_kernel, n, hpd, hd, group, chunk,...  174 us

profile of v6, /device:TPU:21, one launch (start us, length us, event | category | flops | bytes accessed | tf_op | source)
XLA Modules:
  0.0 175.4 jit_solution(1657110862781974366)
XLA Ops:
  0.0 174.3 %layer.1 = bf16[256,2560]{1,0:T(8,128)(2,1)S(1)} custom-call(bf16[256,2560]{1,0:T(8,128)(2,1)} %xin_ref.1, f32[20,128]{1,0:T(8,128)} %bitcast.4, f32[20,128]{1,0:T(8,128)} %bitcast.5, f32[2,40,256]{2,1,0:T(8,128)} %constant.4.clone.angle_ref, f32[2,40,128]{2,1,0:T(8,128)} %constant.5.clone.start_ref, bf16[2560,7680]{1,0:T(8,128)(2,1)} %wqkv_ref.1, ...), custom_call_target="tpu_custom_call" | custom-call | tf_op jit(solution)/shard_map/layer/pallas_call | solution.py:483
  174.3 1.1 copy.12
